TPU v7x, 32 devices: a whole 2x2x4 slice. The times are simulated.
32 devices in a mesh: dp: 2 (over y), expert: 4 (over z), tensor: 4 (over x, core).
Axes of the slice: x: 2, y: 2, z: 4, core: 2. Of those that a mesh axis runs over, the one named last changes fastest.
Arguments:
- grad_out: bfloat16 [1024, 6144], P(('dp', 'expert'), 'tensor'), may hold values from -0.1875 to 0.1875
- expert_ids: int32 [1024, 2], P(('dp', 'expert')), may hold values from 0 to 3, all different within a row; in each aligned block of 128 rows (0 to 127, 128 to 255, ...) at most 64 rows name the same one
- route_gates: float32 [1024, 2], P(('dp', 'expert')), may hold values from 0.1 to 1
- saved_hidden: bfloat16 [4, 256, 16384], P('expert', 'dp', 'tensor'), may hold values from -6 to 6
Outputs:
- weight_grad: bfloat16 [4, 16384, 6144], P('expert', 'tensor', 'dp')
Inputs may be any that keep to these rules, and one draw needn't show every extreme that they name: `expert_ids`: each row names 2 different experts. Among the rows of one device no expert is named by more than 64 rows, and every expert is named somewhere.
All inputs are finite; a program needn't handle non-finite values.
Results may differ from a plain program's by a relative error of at most 0.0049.
Values may be sent and summed in bfloat16 or wider, within the bound.
A program may use at most 128 MiB of HBM per device.

v0:
```python
import functools

import jax
import jax.numpy as jnp
from jax import lax
from jax.experimental import pallas as pl
from jax.experimental.pallas import tpu as pltpu
from jax.sharding import PartitionSpec as P

TOP = 2
CAP = 32
MESH = pl.DeviceIdType.MESH
TN = (((0,), (0,)), ((), ()))


def slot_table(expert_ids, route_gates, expert_count):
    routes = expert_ids.reshape(-1)
    weights = route_gates.reshape(-1)
    onehot = (routes[:, None] == jnp.arange(expert_count, dtype=jnp.int32)[None, :]).astype(
        jnp.int32
    )
    before = jnp.cumsum(onehot, axis=0) - onehot
    rank = jnp.sum(before * onehot, axis=1)
    target = jnp.where(rank < CAP, routes * CAP + rank, -1)
    match = jnp.arange(expert_count * CAP, dtype=jnp.int32)[:, None] == target[None, :]
    chosen = match.reshape(expert_count * CAP, -1, TOP).any(axis=2)
    slot_gate = jnp.sum(
        jnp.where(match, weights[None, :], jnp.zeros_like(weights)[None, :]), axis=1
    )
    return (chosen.astype(jnp.bfloat16), slot_gate)


def plain(grad_out, expert_ids, route_gates, saved_hidden):
    data_count = lax.axis_size("dp")
    expert_count = lax.axis_size("expert")
    chosen, slot_gate = slot_table(expert_ids, route_gates, expert_count)
    width = grad_out.shape[1] * lax.axis_size("tensor")
    block_width = width // data_count
    complete = lax.all_gather(grad_out, "tensor", axis=1, tiled=True)
    parted = complete.reshape(complete.shape[0], data_count, block_width)
    picked = jnp.einsum("st,tdk->dsk", chosen, parted, preferred_element_type=jnp.float32)
    outgoing = (picked * slot_gate[None, :, None]).astype(jnp.bfloat16)
    outgoing = outgoing.reshape(data_count * expert_count, CAP, block_width)
    arrived = lax.all_to_all(outgoing, ("dp", "expert"), split_axis=0, concat_axis=0, tiled=True)
    received = arrived.reshape(-1, block_width)
    summed = lax.dot_general(
        lax.all_gather(saved_hidden[0], "dp", axis=0, tiled=True),
        received,
        TN,
        preferred_element_type=jnp.float32,
    )
    return summed.astype(jnp.bfloat16)[None]


def slot_rows(ids, gates, grad, experts):
    tokens = ids.shape[1]
    named, gate, rank = [], [], []
    for e in range(experts):
        first = (ids[0:1, :] == e).astype(jnp.float32)
        second = (ids[1:2, :] == e).astype(jnp.float32)
        named.append(jnp.broadcast_to(first + second, (CAP, tokens)))
        gate.append(jnp.broadcast_to(first * gates[0:1, :] + second * gates[1:2, :], (CAP, tokens)))
        rank.append(lax.broadcasted_iota(jnp.int32, (CAP, tokens), 0))
    named = jnp.concatenate(named, axis=0)
    gate = jnp.concatenate(gate, axis=0)
    rank = jnp.concatenate(rank, axis=0).astype(jnp.float32)
    row = lax.broadcasted_iota(jnp.int32, (tokens, tokens), 0)
    column = lax.broadcasted_iota(jnp.int32, (tokens, tokens), 1)
    earlier = jnp.where(row < column, 1.0, 0.0).astype(jnp.bfloat16)
    before = jnp.dot(named.astype(jnp.bfloat16), earlier, preferred_element_type=jnp.float32)
    chosen = jnp.where(before == rank, named, 0.0)
    slot_gate = jnp.sum(chosen * gate, axis=1, keepdims=True)
    picked = jnp.dot(chosen.astype(jnp.bfloat16), grad, preferred_element_type=jnp.float32)
    return (picked * slot_gate).astype(jnp.bfloat16)


def exchange(
    D, E, T, cuts, ids_ref, gates_ref, grad_ref, hidden_ref, g_ref, other_ref, slots,
    h_send, h_recv, s1, r1, s2, r2, s3, r3,
):
    d, e, t = lax.axis_index("dp"), lax.axis_index("expert"), lax.axis_index("tensor")
    q = T // D
    x, c = t // q, t % q
    cols = grad_ref.shape[1]
    W = cols // D
    rows = hidden_ref.shape[0]

    def hidden_copy(n, i):
        lo, hi = cuts[i], cuts[i + 1]
        return pltpu.make_async_remote_copy(
            src_ref=hidden_ref.at[pl.ds(lo, hi - lo), :],
            dst_ref=other_ref.at[pl.ds((D - n - 1) * rows + lo, hi - lo), :],
            send_sem=h_send.at[n - 1, i],
            recv_sem=h_recv.at[D - n - 1, i],
            device_id=((d + n) % D, e, t),
            device_id_type=MESH,
        )

    for n in range(1, D):
        hidden_copy(n, 0).start()

    slots[...] = slot_rows(ids_ref[...], gates_ref[...], grad_ref[...], E)

    def place(r, source, x_at, c_at):
        return g_ref.at[
            pl.ds(pl.multiple_of(r * (E * CAP) + source * CAP, CAP), CAP),
            pl.ds(pl.multiple_of(c_at * cols + x_at * W, 128), W),
        ]

    def first(j, m):
        e2, x2 = (e + j) % E, (x + m) % D
        r = (d - x + D) % D
        src = slots.at[
            pl.ds(pl.multiple_of(e2 * CAP, CAP), CAP), pl.ds(pl.multiple_of(x2 * W, 128), W)
        ]
        return src, place(r, e, x2, c), r1.at[r, (E - j) % E], (x, e2, x2 * q + c)

    def first_remote(j, m):
        src, dst, sem, to = first(j, m)
        return pltpu.make_async_remote_copy(
            src_ref=src, dst_ref=dst, send_sem=s1.at[j, m], recv_sem=sem,
            device_id=to, device_id_type=MESH,
        )

    def first_local():
        src = slots.at[
            pl.ds(pl.multiple_of(e * CAP, CAP), CAP), pl.ds(pl.multiple_of(x * W, 128), W)
        ]
        return pltpu.make_async_copy(src, place(0, e, x, c), r1.at[0, 0])

    order = sorted(range(E), key=lambda j: -min(j, E - j))
    for j in order:
        for m in range(D):
            if j == 0 and m == 0:
                pl.when(x == d)(lambda: first_local().start())
                pl.when(x != d)(lambda: first_remote(0, 0).start())
            else:
                first_remote(j, m).start()

    for i in range(1, len(cuts) - 1):
        for n in range(1, D):
            hidden_copy(n, i).start()

    def along(n, r, k):
        here = place(r, (e + k) % E, x, c)
        return pltpu.make_async_remote_copy(
            src_ref=here, dst_ref=here, send_sem=s2.at[n - 1, r, k], recv_sem=r2.at[D - n - 1, r, k],
            device_id=(d, e, ((x + n) % D) * q + c), device_id_type=MESH,
        )

    def along_arrived(n, r, k):
        here = place(r, (e + k) % E, (x + n) % D, c)
        return pltpu.make_async_remote_copy(
            src_ref=here, dst_ref=here, send_sem=s2.at[n - 1, r, k], recv_sem=r2.at[n - 1, r, k],
            device_id=(d, e, ((x + n) % D) * q + c), device_id_type=MESH,
        )

    def across(p, n, r, k):
        here = place(r, (e + k) % E, (x + n) % D, c)
        return pltpu.make_async_remote_copy(
            src_ref=here, dst_ref=here, send_sem=s3.at[p - 1, n, r, k],
            recv_sem=r3.at[q - p - 1, n, r, k],
            device_id=(d, e, x * q + (c + p) % q), device_id_type=MESH,
        )

    def across_arrived(p, n, r, k):
        here = place(r, (e + k) % E, (x + n) % D, (c + p) % q)
        return pltpu.make_async_remote_copy(
            src_ref=here, dst_ref=here, send_sem=s3.at[p - 1, n, r, k],
            recv_sem=r3.at[p - 1, n, r, k],
            device_id=(d, e, x * q + (c + p) % q), device_id_type=MESH,
        )

    def first_arrived(r, k):
        here = place(r, (e + k) % E, x, c)
        return pltpu.make_async_remote_copy(
            src_ref=here, dst_ref=here, send_sem=s1.at[0, 0], recv_sem=r1.at[r, k],
            device_id=((d + r) % D, (e + k) % E, d * q + c), device_id_type=MESH,
        )

    blocks = [(r, k) for k in reversed(order) for r in range(D)]
    for r, k in blocks:
        if r == 0 and k == 0:
            pl.when(x == d)(lambda: first_local().wait())
            pl.when(x != d)(lambda: first_arrived(0, 0).wait_recv())
        else:
            first_arrived(r, k).wait_recv()
        for n in range(1, D):
            along(n, r, k).start()
        for p in range(1, q):
            across(p, 0, r, k).start()
    for r, k in blocks:
        for n in range(1, D):
            along_arrived(n, r, k).wait_recv()
            for p in range(1, q):
                across(p, n, r, k).start()
    for r, k in blocks:
        for p in range(1, q):
            for n in range(D):
                across_arrived(p, n, r, k).wait_recv()
    for j in order:
        for m in range(D):
            if j == 0 and m == 0:
                pl.when(x != d)(lambda: first_remote(0, 0).wait_send())
            else:
                first_remote(j, m).wait_send()
    for r, k in blocks:
        for n in range(1, D):
            along(n, r, k).wait_send()
        for p in range(1, q):
            for n in range(D):
                across(p, n, r, k).wait_send()
    for i in range(len(cuts) - 1):
        for n in range(1, D):
            hidden_copy(n, i).wait_send()
            pltpu.make_async_remote_copy(
                src_ref=hidden_ref.at[pl.ds(cuts[i], cuts[i + 1] - cuts[i]), :],
                dst_ref=other_ref.at[pl.ds((n - 1) * rows + cuts[i], cuts[i + 1] - cuts[i]), :],
                send_sem=h_send.at[n - 1, i],
                recv_sem=h_recv.at[n - 1, i],
                device_id=((d + n) % D, e, t),
                device_id_type=MESH,
            ).wait_recv()


def product(strip, own_ref, other_ref, g_ref, o_ref):
    hidden = jnp.concatenate([own_ref[...], other_ref[...]], axis=0)
    for lo in range(0, g_ref.shape[1], strip):
        o_ref[:, lo:lo + strip] = lax.dot_general(
            hidden, g_ref[:, lo:lo + strip], TN, preferred_element_type=jnp.float32
        ).astype(o_ref.dtype)


def local(grad_out, expert_ids, route_gates, saved_hidden):
    D, E, T = lax.axis_size("dp"), lax.axis_size("expert"), lax.axis_size("tensor")
    tokens, cols = grad_out.shape
    rows, units = saved_hidden.shape[1:]
    depth = D * E * CAP
    width = cols * T // D
    tile, strip = 1024, 1024
    if T % D or cols % (128 * D) or units % tile or width % strip or rows != E * CAP or tokens % 128:
        return plain(grad_out, expert_ids, route_gates, saved_hidden)
    q = T // D
    hidden = saved_hidden[0]
    cuts = (0, rows // 4, rows)
    pieces = len(cuts) - 1
    vmem = pl.BlockSpec(memory_space=pltpu.VMEM)
    hbm = pl.BlockSpec(memory_space=pl.ANY)
    dma = pltpu.SemaphoreType.DMA
    g, other = pl.pallas_call(
        functools.partial(exchange, D, E, T, cuts),
        out_shape=(
            jax.ShapeDtypeStruct((depth, width), jnp.bfloat16),
            jax.ShapeDtypeStruct(((D - 1) * rows, units), jnp.bfloat16),
        ),
        in_specs=[vmem, vmem, vmem, hbm],
        out_specs=(vmem, hbm),
        scratch_shapes=[
            pltpu.VMEM((E * CAP, cols), jnp.bfloat16),
            dma((D - 1, pieces)), dma((D - 1, pieces)),
            dma((E, D)), dma((D, E)),
            dma((D - 1, D, E)), dma((D - 1, D, E)),
            dma((q - 1, D, D, E)), dma((q - 1, D, D, E)),
        ],
        compiler_params=pltpu.CompilerParams(has_side_effects=True),
    )(expert_ids.T, route_gates.T, grad_out, hidden)
    summed = pl.pallas_call(
        functools.partial(product, strip),
        grid=(units // tile,),
        out_shape=jax.ShapeDtypeStruct((units, width), jnp.bfloat16),
        in_specs=[
            pl.BlockSpec((rows, tile), lambda i: (0, i)),
            pl.BlockSpec(((D - 1) * rows, tile), lambda i: (0, i)),
            pl.BlockSpec((depth, width), lambda i: (0, 0)),
        ],
        out_specs=pl.BlockSpec((tile, width), lambda i: (i, 0)),
        compiler_params=pltpu.CompilerParams(dimension_semantics=("arbitrary",)),
    )(hidden, other, g)
    return summed[None]


def solution(mesh):
    in_specs = (
        P(("dp", "expert"), "tensor"),
        P(("dp", "expert"), None),
        P(("dp", "expert"), None),
        P("expert", "dp", "tensor"),
    )
    out_specs = P("expert", "tensor", "dp")
    return jax.shard_map(local, mesh=mesh, in_specs=in_specs, out_specs=out_specs, check_vma=False)
```

profile of v0, /device:TPU:0, one launch (start us, length us, event | category | flops | bytes accessed | tf_op | source)
XLA Modules:
  0.0 52.5 jit_solution(13670852479103348910)
XLA Ops:
  0.0 39.8 %shard_map.46 = (bf16[256,3072]{1,0:T(8,128)(2,1)}, bf16[128,4096]{1,0:T(8,128)(2,1)}) custom-call(s32[2,128]{1,0:T(2,128)} %bitcast.6, f32[2,128]{1,0:T(2,128)} %bitcast.7, bf16[128,1536]{1,0:T(8,128)(2,1)} %grad_ref.1, bf16[128,4096]{1,0:T(8,128)(2,1)} %bitcast.4), custom_call_target="tpu_custom_call" | custom-call | tf_op jit(solution)/shard_map/pallas_call | solution.py:250
  39.8 12.8 %shard_map.47 = bf16[4096,3072]{1,0:T(8,128)(2,1)} custom-call(bf16[128,4096]{1,0:T(8,128)(2,1)} %bitcast.5, bf16[128,4096]{1,0:T(8,128)(2,1)} %get-tuple-element.7.other_ref, bf16[256,3072]{1,0:T(8,128)(2,1)} %get-tuple-element.8.g_ref), custom_call_target="tpu_custom_call" | custom-call | tf_op jit(solution)/shard_map/pallas_call | solution.py:267
where the time goes:
time: 52.7 us; the launch traced here: 52.5 us
  Pallas kernels  52.5 us (100%)
    pallas_call x1, Pallas kernels, local(): pl.pallas_call(functools.partial(exchange, D, E, T, cuts), out_shape=(jax...  39.8 us
    pallas_call x1, Pallas kernels, local(): pl.pallas_call(functools.partial(product, strip), grid=(units // tile,),...  12.8 us

commit v1 on v0

--- a/solution.py
+++ b/solution.py
@@ -96,10 +96,28 @@
             device_id_type=MESH,
         )
 
+    barrier = pltpu.get_barrier_semaphore()
+
+    def greet(to):
+        pl.semaphore_signal(barrier, inc=1, device_id=to, device_id_type=MESH)
+
+    for n in range(1, D):
+        greet(((d + n) % D, e, t))
+        greet((d, e, ((x + n) % D) * q + c))
+    for p in range(1, q):
+        greet((d, e, x * q + (c + p) % q))
+    for n in range(D):
+        for j in range(E):
+            to = ((x + n) % D, (e + j) % E, d * q + c)
+            if n == 0 and j == 0:
+                pl.when(x != d)(functools.partial(greet, to))
+            else:
+                greet(to)
+    slots[...] = slot_rows(ids_ref[...], gates_ref[...], grad_ref[...], E)
+    pl.semaphore_wait(barrier, 2 * (D - 1) + q - 1 + D * E - jnp.where(x == d, 1, 0))
+
     for n in range(1, D):
         hidden_copy(n, 0).start()
-
-    slots[...] = slot_rows(ids_ref[...], gates_ref[...], grad_ref[...], E)
 
     def place(r, source, x_at, c_at):
         return g_ref.at[
@@ -262,7 +280,7 @@
             dma((D - 1, D, E)), dma((D - 1, D, E)),
             dma((q - 1, D, D, E)), dma((q - 1, D, D, E)),
         ],
-        compiler_params=pltpu.CompilerParams(has_side_effects=True),
+        compiler_params=pltpu.CompilerParams(has_side_effects=True, collective_id=0),
     )(expert_ids.T, route_gates.T, grad_out, hidden)
     summed = pl.pallas_call(
         functools.partial(product, strip),

time: 52.7 us -> 50.4 us (0.956)
  Pallas kernels: 52.5 us -> 50.2 us
    pallas_call x1, Pallas kernels: 39.8 us -> 37.5 us  [local(): pl.pallas_call(functools.partial(exchange, D, E, T, cuts), out_shape=(jax...]
where the time goes in v1:
time: 50.4 us; the launch traced here: 50.2 us
  Pallas kernels  50.2 us (100%)
    pallas_call x1, Pallas kernels, local(): pl.pallas_call(functools.partial(exchange, D, E, T, cuts), out_shape=(jax...  37.5 us
    pallas_call x1, Pallas kernels, local(): pl.pallas_call(functools.partial(product, strip), grid=(units // tile,),...  12.8 us

profile of v1, /device:TPU:0, one launch (start us, length us, event | category | flops | bytes accessed | tf_op | source)
XLA Modules:
  0.0 50.2 jit_solution(8345109979899947493)
XLA Ops:
  0.0 37.5 %shard_map.46 = (bf16[256,3072]{1,0:T(8,128)(2,1)}, bf16[128,4096]{1,0:T(8,128)(2,1)}) custom-call(s32[2,128]{1,0:T(2,128)} %bitcast.6, f32[2,128]{1,0:T(2,128)} %bitcast.7, bf16[128,1536]{1,0:T(8,128)(2,1)} %grad_ref.1, bf16[128,4096]{1,0:T(8,128)(2,1)} %bitcast.4), custom_call_target="tpu_custom_call" | custom-call | tf_op jit(solution)/shard_map/pallas_call | solution.py:268
  37.5 12.8 %shard_map.47 = bf16[4096,3072]{1,0:T(8,128)(2,1)} custom-call(bf16[128,4096]{1,0:T(8,128)(2,1)} %bitcast.5, bf16[128,4096]{1,0:T(8,128)(2,1)} %get-tuple-element.7.other_ref, bf16[256,3072]{1,0:T(8,128)(2,1)} %get-tuple-element.8.g_ref), custom_call_target="tpu_custom_call" | custom-call | tf_op jit(solution)/shard_map/pallas_call | solution.py:285

commit v2 on v1

--- a/solution.py
+++ b/solution.py
@@ -11,6 +11,7 @@
 CAP = 32
 MESH = pl.DeviceIdType.MESH
 TN = (((0,), (0,)), ((), ()))
+EARLY, INSIDE, LATER = 1, 4, (2, 1, 1)
 
 
 def slot_table(expert_ids, route_gates, expert_count):
@@ -75,26 +76,35 @@
 
 
 def exchange(
-    D, E, T, cuts, ids_ref, gates_ref, grad_ref, hidden_ref, g_ref, other_ref, slots,
-    h_send, h_recv, s1, r1, s2, r2, s3, r3,
+    D, E, T, lo, hi, later, ids_ref, gates_ref, grad_ref, hidden_ref, g_ref, other_ref, *rest
 ):
+    parts = rest[:len(later)]
+    (slots, staged, p_in, p_out, h_send, h_recv, s1, r1, s2, r2, s3, r3) = rest[len(later):]
     d, e, t = lax.axis_index("dp"), lax.axis_index("expert"), lax.axis_index("tensor")
     q = T // D
     x, c = t // q, t % q
     cols = grad_ref.shape[1]
     W = cols // D
-    rows = hidden_ref.shape[0]
-
-    def hidden_copy(n, i):
-        lo, hi = cuts[i], cuts[i + 1]
-        return pltpu.make_async_remote_copy(
-            src_ref=hidden_ref.at[pl.ds(lo, hi - lo), :],
-            dst_ref=other_ref.at[pl.ds((D - n - 1) * rows + lo, hi - lo), :],
-            send_sem=h_send.at[n - 1, i],
-            recv_sem=h_recv.at[D - n - 1, i],
-            device_id=((d + n) % D, e, t),
+
+    def hidden_copy():
+        return pltpu.make_async_remote_copy(
+            src_ref=hidden_ref.at[:, pl.ds(lo, hi - lo)],
+            dst_ref=other_ref,
+            send_sem=h_send,
+            recv_sem=h_recv,
+            device_id=((d + 1) % D, e, t),
             device_id_type=MESH,
         )
+
+    def stage_in(i):
+        at, size = later[i]
+        return pltpu.make_async_copy(
+            hidden_ref.at[:, pl.ds(at, size)], staged.at[:, pl.ds(at - hi, size)], p_in.at[i]
+        )
+
+    def stage_out(i):
+        at, size = later[i]
+        return pltpu.make_async_copy(staged.at[:, pl.ds(at - hi, size)], parts[i], p_out.at[i])
 
     barrier = pltpu.get_barrier_semaphore()
 
@@ -113,11 +123,10 @@
                 pl.when(x != d)(functools.partial(greet, to))
             else:
                 greet(to)
+    for i in range(len(later)):
+        stage_in(i).start()
     slots[...] = slot_rows(ids_ref[...], gates_ref[...], grad_ref[...], E)
     pl.semaphore_wait(barrier, 2 * (D - 1) + q - 1 + D * E - jnp.where(x == d, 1, 0))
-
-    for n in range(1, D):
-        hidden_copy(n, 0).start()
 
     def place(r, source, x_at, c_at):
         return g_ref.at[
@@ -155,9 +164,10 @@
             else:
                 first_remote(j, m).start()
 
-    for i in range(1, len(cuts) - 1):
-        for n in range(1, D):
-            hidden_copy(n, i).start()
+    hidden_copy().start()
+    for i in range(len(later)):
+        stage_in(i).wait()
+        stage_out(i).start()
 
     def along(n, r, k):
         here = place(r, (e + k) % E, x, c)
@@ -228,25 +238,75 @@
         for p in range(1, q):
             for n in range(D):
                 across(p, n, r, k).wait_send()
-    for i in range(len(cuts) - 1):
-        for n in range(1, D):
-            hidden_copy(n, i).wait_send()
-            pltpu.make_async_remote_copy(
-                src_ref=hidden_ref.at[pl.ds(cuts[i], cuts[i + 1] - cuts[i]), :],
-                dst_ref=other_ref.at[pl.ds((n - 1) * rows + cuts[i], cuts[i + 1] - cuts[i]), :],
-                send_sem=h_send.at[n - 1, i],
-                recv_sem=h_recv.at[n - 1, i],
-                device_id=((d + n) % D, e, t),
-                device_id_type=MESH,
-            ).wait_recv()
-
-
-def product(strip, own_ref, other_ref, g_ref, o_ref):
-    hidden = jnp.concatenate([own_ref[...], other_ref[...]], axis=0)
-    for lo in range(0, g_ref.shape[1], strip):
-        o_ref[:, lo:lo + strip] = lax.dot_general(
-            hidden, g_ref[:, lo:lo + strip], TN, preferred_element_type=jnp.float32
-        ).astype(o_ref.dtype)
+    for i in range(len(later)):
+        stage_out(i).wait()
+    hidden_copy().wait()
+
+
+def product(base, spans, tile, strip, slots, own_ref, *refs):
+    others = refs[:len(spans)]
+    g_ref = refs[len(spans)]
+    o_ref, hv, gv, ob, hs, gs, os = refs[-7:]
+    rows, width = own_ref.shape[0], g_ref.shape[1]
+    tiles = [(o, at) for o, size in zip(others, spans) for at in range(0, size, tile)]
+    count = len(tiles)
+    depth = min(slots, count)
+
+    def load(k):
+        other, at = tiles[k]
+        return (
+            pltpu.make_async_copy(
+                own_ref.at[:, pl.ds(base + k * tile, tile)], hv.at[k, pl.ds(0, rows), :], hs.at[k, 0]
+            ),
+            pltpu.make_async_copy(
+                other.at[:, pl.ds(at, tile)], hv.at[k, pl.ds(rows, rows), :], hs.at[k, 1]
+            ),
+        )
+
+    def loaded(k):
+        for i in range(2):
+            pltpu.make_async_copy(
+                own_ref.at[:, pl.ds(0, tile)], hv.at[k, pl.ds(i * rows, rows), :], hs.at[k, i]
+            ).wait()
+
+    pieces = [
+        pltpu.make_async_copy(g_ref.at[:, pl.ds(at, strip)], gv.at[:, pl.ds(at, strip)], gs.at[i])
+        for i, at in enumerate(range(0, width, strip))
+    ]
+    for k in range(count):
+        for copy in load(k):
+            copy.start()
+        if k == 0:
+            for copy in pieces:
+                copy.start()
+
+    def leave(k):
+        return pltpu.make_async_copy(
+            ob.at[k % depth],
+            o_ref.at[pl.ds(pl.multiple_of(base + k * tile, tile), tile), :],
+            os.at[k % depth],
+        )
+
+    def step(k, opening=False, reuse=False):
+        loaded(k)
+        if reuse:
+            leave(k - depth).wait()
+        hidden = hv[k]
+        for i, at in enumerate(range(0, width, strip)):
+            if opening:
+                pieces[i].wait()
+            ob[k % depth, :, at:at + strip] = lax.dot_general(
+                hidden, gv[:, at:at + strip], TN, preferred_element_type=jnp.float32
+            ).astype(ob.dtype)
+        leave(k).start()
+
+    step(0, opening=True)
+    if depth > 1:
+        pl.loop(1, depth)(lambda k: step(k))
+    if count > depth:
+        pl.loop(depth, count)(lambda k: step(k, reuse=True))
+    for k in range(count - depth, count):
+        leave(k).wait()
 
 
 def local(grad_out, expert_ids, route_gates, saved_hidden):
@@ -255,46 +315,77 @@
     rows, units = saved_hidden.shape[1:]
     depth = D * E * CAP
     width = cols * T // D
-    tile, strip = 1024, 1024
-    if T % D or cols % (128 * D) or units % tile or width % strip or rows != E * CAP or tokens % 128:
+    tile, strip = 512, 1024
+    if (
+        D != 2 or T % D or cols % (128 * D) or units % (8 * tile) or width % strip
+        or rows != E * CAP or tokens % 128
+    ):
         return plain(grad_out, expert_ids, route_gates, saved_hidden)
     q = T // D
     hidden = saved_hidden[0]
-    cuts = (0, rows // 4, rows)
-    pieces = len(cuts) - 1
+    share = units // 8
+    ahead, stop = EARLY * share, INSIDE * share
+    later, at = [], stop
+    for part in LATER:
+        later.append((at, part * share))
+        at += part * share
+    later = tuple(later)
     vmem = pl.BlockSpec(memory_space=pltpu.VMEM)
     hbm = pl.BlockSpec(memory_space=pl.ANY)
     dma = pltpu.SemaphoreType.DMA
-    g, other = pl.pallas_call(
-        functools.partial(exchange, D, E, T, cuts),
+    bf16 = jnp.bfloat16
+    swap = [(0, 1), (1, 0)]
+    first = lax.ppermute(hidden[:, :ahead], "dp", swap)
+    g, other, *parts = pl.pallas_call(
+        functools.partial(exchange, D, E, T, ahead, stop, later),
         out_shape=(
-            jax.ShapeDtypeStruct((depth, width), jnp.bfloat16),
-            jax.ShapeDtypeStruct(((D - 1) * rows, units), jnp.bfloat16),
+            jax.ShapeDtypeStruct((depth, width), bf16),
+            jax.ShapeDtypeStruct((rows, stop - ahead), bf16),
+            *(jax.ShapeDtypeStruct((rows, size), bf16) for _, size in later),
         ),
         in_specs=[vmem, vmem, vmem, hbm],
-        out_specs=(vmem, hbm),
+        out_specs=(vmem, hbm, *(hbm for _ in later)),
         scratch_shapes=[
-            pltpu.VMEM((E * CAP, cols), jnp.bfloat16),
-            dma((D - 1, pieces)), dma((D - 1, pieces)),
+            pltpu.VMEM((E * CAP, cols), bf16),
+            pltpu.VMEM((rows, units - stop), bf16),
+            dma((len(later),)), dma((len(later),)),
+            dma, dma,
             dma((E, D)), dma((D, E)),
             dma((D - 1, D, E)), dma((D - 1, D, E)),
             dma((q - 1, D, D, E)), dma((q - 1, D, D, E)),
         ],
+        cost_estimate=pl.CostEstimate(flops=2 * 10**10, bytes_accessed=2**22, transcendentals=0),
         compiler_params=pltpu.CompilerParams(has_side_effects=True, collective_id=0),
     )(expert_ids.T, route_gates.T, grad_out, hidden)
-    summed = pl.pallas_call(
-        functools.partial(product, strip),
-        grid=(units // tile,),
-        out_shape=jax.ShapeDtypeStruct((units, width), jnp.bfloat16),
-        in_specs=[
-            pl.BlockSpec((rows, tile), lambda i: (0, i)),
-            pl.BlockSpec(((D - 1) * rows, tile), lambda i: (0, i)),
-            pl.BlockSpec((depth, width), lambda i: (0, 0)),
-        ],
-        out_specs=pl.BlockSpec((tile, width), lambda i: (i, 0)),
-        compiler_params=pltpu.CompilerParams(dimension_semantics=("arbitrary",)),
-    )(hidden, other, g)
-    return summed[None]
+    arrived = [lax.ppermute(part, "dp", swap) for part in parts]
+
+    def run(base, others, out):
+        spans = tuple(o.shape[1] for o in others)
+        count = sum(spans) // tile
+        slots = min(4, count)
+        return pl.pallas_call(
+            functools.partial(product, base, spans, tile, strip, slots),
+            out_shape=jax.ShapeDtypeStruct((units, width), bf16),
+            in_specs=[hbm] * (len(others) + 2 + len(out)),
+            out_specs=hbm,
+            scratch_shapes=[
+                pltpu.VMEM((count, 2 * rows, tile), bf16),
+                pltpu.VMEM((depth, width), bf16),
+                pltpu.VMEM((slots, tile, width), bf16),
+                dma((count, 2)), dma((width // strip,)), dma((slots,)),
+            ],
+            input_output_aliases={len(others) + 2: 0} if out else {},
+            cost_estimate=pl.CostEstimate(
+                flops=2 * depth * width * count * tile,
+                bytes_accessed=2 * width * count * tile,
+                transcendentals=0,
+            ),
+        )(hidden, *others, g, *out)
+
+    out = run(0, (first, other), ())
+    for (at, _), part in zip(later, arrived):
+        out = run(at, (part,), (out,))
+    return out[None]
 
 
 def solution(mesh):

time: 50.4 us -> 57.3 us (1.14)
  Pallas kernels: 50.2 us -> 43.8 us
  starting transfers between devices: 0 us -> 5.23 us
  waiting for transfers between devices: 0 us -> 4.16 us
  local copies, waits for them, and re-layouts: 0 us -> 3.55 us
    pallas_call x2 -> x5, Pallas kernels: 50.2 us -> 43.8 us  [the longest x1 22.3 us: local(): pl.pallas_call(functools.partial(exchange, D, E, T, ahead, stop, later),...]
    ppermute x0 -> x4, starting transfers between devices: none -> 5.23 us  [the longest x1 3.06 us: local(): first = lax.ppermute(hidden[:, :ahead], 'dp', swap)]
    ppermute x0 -> x4, waiting for transfers between devices: none -> 4.16 us  [the longest x3 4.16 us: local(): arrived = [lax.ppermute(part, 'dp', swap) for part in parts]]
    unnamed x0 -> x8, local copies, waits for them, and re-layouts: none -> 2.64 us
    slice x0 -> x1, local copies, waits for them, and re-layouts: none -> 0.91 us  [local(): first = lax.ppermute(hidden[:, :ahead], 'dp', swap)]
  transfers between devices with their start and end apart: 0 -> 4, of which waited for: 0 -> 1; matrix products, arithmetic and copies ran while one was open for 0% -> 0% of each run, Pallas kernels for 0% -> 69%
where the time goes in v2:
time: 57.3 us; the launch traced here: 56.8 us
  Pallas kernels  43.8 us (76%)
  starting transfers between devices  5.23 us (9%)
  waiting for transfers between devices  4.16 us (7%)
  local copies, waits for them, and re-layouts  3.55 us (6%)
    pallas_call x1, Pallas kernels, local(): pl.pallas_call(functools.partial(exchange, D, E, T, ahead, stop, later),...  22.3 us
    pallas_call x4, Pallas kernels, run(): pl.pallas_call(functools.partial(product, base, spans, tile, strip, slots...  21.5 us
    ppermute x3, waiting for transfers between devices, local(): arrived = [lax.ppermute(part, 'dp', swap) for part in parts]  4.16 us
    ppermute x1, starting transfers between devices, local(): first = lax.ppermute(hidden[:, :ahead], 'dp', swap)  3.06 us
    unnamed x8, local copies, waits for them, and re-layouts  2.64 us
    ppermute x3, starting transfers between devices, local(): arrived = [lax.ppermute(part, 'dp', swap) for part in parts]  2.17 us
  transfers between devices with their start and end apart: 4, of which 1 were waited for; matrix products, arithmetic and copies ran while one was open for 0% of the time, Pallas kernels for 69%

profile of v2, /device:TPU:0, one launch (start us, length us, event | category | flops | bytes accessed | tf_op | source)
XLA Modules:
  0.0 56.8 jit_solution(1369485270289533280)
XLA Ops:
  0.0 0.9 %slice.4 = bf16[128,512]{1,0:T(8,128)(2,1)S(1)} slice(bf16[128,4096]{1,0:T(8,128)(2,1)} %bitcast.4), slice={[0:128], [0:512]} | slice | bytes 262144 | tf_op jit(solution)/shard_map/slice | solution.py:338
  0.9 3.1 %collective-permute-start.3 = (bf16[128,512]{1,0:T(8,128)(2,1)S(1)}, bf16[128,512]{1,0:T(8,128)(2,1)S(1)}, u32[]{:S(2)}, u32[]{:S(2)}) collective-permute-start(bf16[128,512]{1,0:T(8,128)(2,1)S(1)} %slice.4), channel_id=1, source_target_pairs={{0,16},{16,0},{1,17},{17,1},{2,18},{18,2},{3,19},{19,3},{4,20},{20... | collective-permute-start | bytes 393224 | tf_op jit(solution)/shard_map/ppermute | solution.py:338
  4.0 22.3 %shard_map.46 = (bf16[256,3072]{1,0:T(8,128)(2,1)}, bf16[128,1536]{1,0:T(8,128)(2,1)}, bf16[128,1024]{1,0:T(8,128)(2,1)}, bf16[128,512]{1,0:T(8,128)(2,1)}, bf16[128,512]{1,0:T(8,128)(2,1)}) custom-call(s32[2,128]{1,0:T(2,128)} %bitcast.10, f32[2,128]{1,0:T(2,128)} %bitcast.11, bf16[128,1536]{1,0:T(8,128)(2,1)} %grad_ref.1, bf16[128,4096]{1,0:T(8,128)(2,1)} %bitcast.5), custom_call_target="tpu_custom_call" | custom-call | flops 20000000000 | bytes 4194304 | tf_op jit(solution)/shard_map/pallas_call | solution.py:339
  26.3 0.1 collective-permute-start
  26.4 2.0 %collective-permute-start.1 = (bf16[128,512]{1,0:T(8,128)(2,1)}, bf16[128,512]{1,0:T(8,128)(2,1)S(1)}, u32[]{:S(2)}, u32[]{:S(2)}) collective-permute-start(bf16[128,512]{1,0:T(8,128)(2,1)} %get-tuple-element.12), channel_id=1, source_target_pairs={{0,16},{16,0},{1,17},{17,1},{2,18},{18,2},{3,19},{19,3},{4,20},{20... | collective-permute-start | bytes 393224 | tf_op jit(solution)/shard_map/ppermute | solution.py:360
  28.4 0.1 collective-permute-start.2
  28.4 0.0 collective-permute-done.3.refs_0_
  28.4 0.0 copy-start.2
  28.5 0.6 %copy-done.2 = bf16[128,512]{1,0:T(8,128)(2,1)} copy-done((bf16[128,512]{1,0:T(8,128)(2,1)}, bf16[128,512]{1,0:T(8,128)(2,1)S(1)}, u32[]{:S(2)}) %copy-start.2) | copy-done | bytes 131096
  29.1 7.5 %shard_map.47.refs_2_ = bf16[4096,3072]{1,0:T(8,128)(2,1)} custom-call(bf16[128,4096]{1,0:T(8,128)(2,1)} %bitcast.6, bf16[128,512]{1,0:T(8,128)(2,1)} %copy-done.2, bf16[128,1536]{1,0:T(8,128)(2,1)} %get-tuple-element.14.refs_1_, bf16[256,3072]{1,0:T(8,128)(2,1)} %get-tuple-element.11.refs_2_.refs_1_), custom_call_target="tpu_custom_call" | custom-call | flops 3221225472 | bytes 12582912 | tf_op jit(solution)/shard_map/pallas_call | solution.py:366
  36.6 4.2 %collective-permute-done.2.refs_0_ = bf16[128,1024]{1,0:T(8,128)(2,1)S(1)} collective-permute-done((bf16[128,1024]{1,0:T(8,128)(2,1)}, bf16[128,1024]{1,0:T(8,128)(2,1)S(1)}, u32[]{:S(2)}, u32[]{:S(2)}) %collective-permute-start.2) | collective-permute-done | bytes 262176 | tf_op jit(solution)/shard_map/ppermute | solution.py:360
  40.8 0.0 copy-start
  40.8 0.7 %copy-done = bf16[128,1024]{1,0:T(8,128)(2,1)} copy-done((bf16[128,1024]{1,0:T(8,128)(2,1)}, bf16[128,1024]{1,0:T(8,128)(2,1)S(1)}, u32[]{:S(2)}) %copy-start) | copy-done | bytes 262168
  41.5 5.3 %shard_map.48.refs_2_ = bf16[4096,3072]{1,0:T(8,128)(2,1)} custom-call(bf16[128,4096]{1,0:T(8,128)(2,1)} %bitcast.7, bf16[128,1024]{1,0:T(8,128)(2,1)} %copy-done, bf16[256,3072]{1,0:T(8,128)(2,1)} %get-tuple-element.11.refs_2_.refs_1_, bf16[4096,3072]{1,0:T(8,128)(2,1)} %shard_map.47.refs_2_), custom_call_target="tpu_custom_call", output_to_operand_aliasing={{}: (3, {})} | custom-call | flops 1610612736 | bytes 6291456 | tf_op jit(solution)/shard_map/pallas_call | solution.py:366
  46.8 0.0 collective-permute-done.1.refs_0_
  46.8 0.0 copy-start.3
  46.8 0.6 %copy-done.3 = bf16[128,512]{1,0:T(8,128)(2,1)} copy-done((bf16[128,512]{1,0:T(8,128)(2,1)}, bf16[128,512]{1,0:T(8,128)(2,1)S(1)}, u32[]{:S(2)}) %copy-start.3) | copy-done | bytes 131096
  47.4 4.3 %shard_map.49.refs_2_ = bf16[4096,3072]{1,0:T(8,128)(2,1)} custom-call(bf16[128,4096]{1,0:T(8,128)(2,1)} %bitcast.8, bf16[128,512]{1,0:T(8,128)(2,1)} %copy-done.3, bf16[256,3072]{1,0:T(8,128)(2,1)} %get-tuple-element.11.refs_2_.refs_1_, bf16[4096,3072]{1,0:T(8,128)(2,1)} %shard_map.48.refs_2_), custom_call_target="tpu_custom_call", output_to_operand_aliasing={{}: (3, {})} | custom-call | flops 805306368 | bytes 3145728 | tf_op jit(solution)/shard_map/pallas_call | solution.py:366
  51.8 0.0 collective-permute-done.refs_0_
  51.8 0.0 copy-start.1
  51.8 0.6 %copy-done.1 = bf16[128,512]{1,0:T(8,128)(2,1)} copy-done((bf16[128,512]{1,0:T(8,128)(2,1)}, bf16[128,512]{1,0:T(8,128)(2,1)S(1)}, u32[]{:S(2)}) %copy-start.1) | copy-done | bytes 131096
  52.5 4.3 %shard_map.50 = bf16[4096,3072]{1,0:T(8,128)(2,1)} custom-call(bf16[128,4096]{1,0:T(8,128)(2,1)} %bitcast.9, bf16[128,512]{1,0:T(8,128)(2,1)} %copy-done.1, bf16[256,3072]{1,0:T(8,128)(2,1)} %get-tuple-element.11.refs_2_.refs_1_, bf16[4096,3072]{1,0:T(8,128)(2,1)} %shard_map.49.refs_2_), custom_call_target="tpu_custom_call", output_to_operand_aliasing={{}: (3, {})} | custom-call | flops 805306368 | bytes 3145728 | tf_op jit(solution)/shard_map/pallas_call | solution.py:366
Async XLA Ops:
  0.9 27.5 %collective-permute-start.3 = (bf16[128,512]{1,0:T(8,128)(2,1)S(1)}, bf16[128,512]{1,0:T(8,128)(2,1)S(1)}, u32[]{:S(2)}, u32[]{:S(2)}) collective-permute-start(bf16[128,512]{1,0:T(8,128)(2,1)S(1)} %slice.4), channel_id=1, source_target_pairs={{0,16},{16,0},{1,17},{17,1},{2,18},{18,2},{3,19},{19,3},{4,20},{20... | collective-permute-start | bytes 393224 | tf_op jit(solution)/shard_map/ppermute | solution.py:338
  26.3 25.5 %collective-permute-start = (bf16[128,512]{1,0:T(8,128)(2,1)}, bf16[128,512]{1,0:T(8,128)(2,1)S(1)}, u32[]{:S(2)}, u32[]{:S(2)}) collective-permute-start(bf16[128,512]{1,0:T(8,128)(2,1)} %get-tuple-element.10), channel_id=1, source_target_pairs={{0,16},{16,0},{1,17},{17,1},{2,18},{18,2},{3,19},{19,3},{4,20},{20... | collective-permute-start | bytes 393224 | tf_op jit(solution)/shard_map/ppermute | solution.py:360
  26.4 20.4 %collective-permute-start.1 = (bf16[128,512]{1,0:T(8,128)(2,1)}, bf16[128,512]{1,0:T(8,128)(2,1)S(1)}, u32[]{:S(2)}, u32[]{:S(2)}) collective-permute-start(bf16[128,512]{1,0:T(8,128)(2,1)} %get-tuple-element.12), channel_id=1, source_target_pairs={{0,16},{16,0},{1,17},{17,1},{2,18},{18,2},{3,19},{19,3},{4,20},{20... | collective-permute-start | bytes 393224 | tf_op jit(solution)/shard_map/ppermute | solution.py:360
  28.4 12.4 %collective-permute-start.2 = (bf16[128,1024]{1,0:T(8,128)(2,1)}, bf16[128,1024]{1,0:T(8,128)(2,1)S(1)}, u32[]{:S(2)}, u32[]{:S(2)}) collective-permute-start(bf16[128,1024]{1,0:T(8,128)(2,1)} %get-tuple-element.13), channel_id=1, source_target_pairs={{0,16},{16,0},{1,17},{17,1},{2,18},{18,2},{3,19},{19,3},{4,20},{20... | collective-permute-start | bytes 786440 | tf_op jit(solution)/shard_map/ppermute | solution.py:360
  28.4 0.6 %copy-start.2 = (bf16[128,512]{1,0:T(8,128)(2,1)}, bf16[128,512]{1,0:T(8,128)(2,1)S(1)}, u32[]{:S(2)}) copy-start(bf16[128,512]{1,0:T(8,128)(2,1)S(1)} %collective-permute-done.3.refs_0_) | copy-start | bytes 393220
  40.8 0.7 %copy-start = (bf16[128,1024]{1,0:T(8,128)(2,1)}, bf16[128,1024]{1,0:T(8,128)(2,1)S(1)}, u32[]{:S(2)}) copy-start(bf16[128,1024]{1,0:T(8,128)(2,1)S(1)} %collective-permute-done.2.refs_0_) | copy-start | bytes 786436
  46.8 0.7 %copy-start.3 = (bf16[128,512]{1,0:T(8,128)(2,1)}, bf16[128,512]{1,0:T(8,128)(2,1)S(1)}, u32[]{:S(2)}) copy-start(bf16[128,512]{1,0:T(8,128)(2,1)S(1)} %collective-permute-done.1.refs_0_) | copy-start | bytes 393220
  51.8 0.7 %copy-start.1 = (bf16[128,512]{1,0:T(8,128)(2,1)}, bf16[128,512]{1,0:T(8,128)(2,1)S(1)}, u32[]{:S(2)}) copy-start(bf16[128,512]{1,0:T(8,128)(2,1)S(1)} %collective-permute-done.refs_0_) | copy-start | bytes 393220

commit v3 on v2

--- a/solution.py
+++ b/solution.py
@@ -7,11 +7,12 @@
 from jax.experimental.pallas import tpu as pltpu
 from jax.sharding import PartitionSpec as P
 
+
 TOP = 2
 CAP = 32
 MESH = pl.DeviceIdType.MESH
 TN = (((0,), (0,)), ((), ()))
-EARLY, INSIDE, LATER = 1, 4, (2, 1, 1)
+EARLY, INSIDE, LATER = 2, 9, (4, 3)
 
 
 def slot_table(expert_ids, route_gates, expert_count):
@@ -79,7 +80,7 @@
     D, E, T, lo, hi, later, ids_ref, gates_ref, grad_ref, hidden_ref, g_ref, other_ref, *rest
 ):
     parts = rest[:len(later)]
-    (slots, staged, p_in, p_out, h_send, h_recv, s1, r1, s2, r2, s3, r3) = rest[len(later):]
+    (slots, p_in, h_send, h_recv, s1, r1, s2, r2, s3, r3) = rest[len(later):]
     d, e, t = lax.axis_index("dp"), lax.axis_index("expert"), lax.axis_index("tensor")
     q = T // D
     x, c = t // q, t % q
@@ -96,15 +97,9 @@
             device_id_type=MESH,
         )
 
-    def stage_in(i):
+    def stage(i):
         at, size = later[i]
-        return pltpu.make_async_copy(
-            hidden_ref.at[:, pl.ds(at, size)], staged.at[:, pl.ds(at - hi, size)], p_in.at[i]
-        )
-
-    def stage_out(i):
-        at, size = later[i]
-        return pltpu.make_async_copy(staged.at[:, pl.ds(at - hi, size)], parts[i], p_out.at[i])
+        return pltpu.make_async_copy(hidden_ref.at[:, pl.ds(at, size)], parts[i], p_in.at[i])
 
     barrier = pltpu.get_barrier_semaphore()
 
@@ -124,7 +119,7 @@
             else:
                 greet(to)
     for i in range(len(later)):
-        stage_in(i).start()
+        stage(i).start()
     slots[...] = slot_rows(ids_ref[...], gates_ref[...], grad_ref[...], E)
     pl.semaphore_wait(barrier, 2 * (D - 1) + q - 1 + D * E - jnp.where(x == d, 1, 0))
 
@@ -165,9 +160,6 @@
                 first_remote(j, m).start()
 
     hidden_copy().start()
-    for i in range(len(later)):
-        stage_in(i).wait()
-        stage_out(i).start()
 
     def along(n, r, k):
         here = place(r, (e + k) % E, x, c)
@@ -239,72 +231,34 @@
             for n in range(D):
                 across(p, n, r, k).wait_send()
     for i in range(len(later)):
-        stage_out(i).wait()
+        stage(i).wait()
     hidden_copy().wait()
 
 
 def product(base, spans, tile, strip, slots, own_ref, *refs):
     others = refs[:len(spans)]
     g_ref = refs[len(spans)]
-    o_ref, hv, gv, ob, hs, gs, os = refs[-7:]
-    rows, width = own_ref.shape[0], g_ref.shape[1]
+    o_ref, ob, os = refs[-3:]
+    width = g_ref.shape[1]
     tiles = [(o, at) for o, size in zip(others, spans) for at in range(0, size, tile)]
     count = len(tiles)
     depth = min(slots, count)
 
-    def load(k):
-        other, at = tiles[k]
-        return (
-            pltpu.make_async_copy(
-                own_ref.at[:, pl.ds(base + k * tile, tile)], hv.at[k, pl.ds(0, rows), :], hs.at[k, 0]
-            ),
-            pltpu.make_async_copy(
-                other.at[:, pl.ds(at, tile)], hv.at[k, pl.ds(rows, rows), :], hs.at[k, 1]
-            ),
-        )
-
-    def loaded(k):
-        for i in range(2):
-            pltpu.make_async_copy(
-                own_ref.at[:, pl.ds(0, tile)], hv.at[k, pl.ds(i * rows, rows), :], hs.at[k, i]
-            ).wait()
-
-    pieces = [
-        pltpu.make_async_copy(g_ref.at[:, pl.ds(at, strip)], gv.at[:, pl.ds(at, strip)], gs.at[i])
-        for i, at in enumerate(range(0, width, strip))
-    ]
-    for k in range(count):
-        for copy in load(k):
-            copy.start()
-        if k == 0:
-            for copy in pieces:
-                copy.start()
-
     def leave(k):
         return pltpu.make_async_copy(
-            ob.at[k % depth],
-            o_ref.at[pl.ds(pl.multiple_of(base + k * tile, tile), tile), :],
-            os.at[k % depth],
-        )
-
-    def step(k, opening=False, reuse=False):
-        loaded(k)
-        if reuse:
+            ob.at[k % depth], o_ref.at[pl.ds(base + k * tile, tile), :], os.at[k % depth]
+        )
+
+    for k, (other, at) in enumerate(tiles):
+        if k >= depth:
             leave(k - depth).wait()
-        hidden = hv[k]
-        for i, at in enumerate(range(0, width, strip)):
-            if opening:
-                pieces[i].wait()
-            ob[k % depth, :, at:at + strip] = lax.dot_general(
-                hidden, gv[:, at:at + strip], TN, preferred_element_type=jnp.float32
+        mine = own_ref[:, base + k * tile:base + (k + 1) * tile]
+        hidden = jnp.concatenate([mine, other[:, at:at + tile]], axis=0)
+        for lo in range(0, width, strip):
+            ob[k % depth, :, lo:lo + strip] = lax.dot_general(
+                hidden, g_ref[:, lo:lo + strip], TN, preferred_element_type=jnp.float32
             ).astype(ob.dtype)
         leave(k).start()
-
-    step(0, opening=True)
-    if depth > 1:
-        pl.loop(1, depth)(lambda k: step(k))
-    if count > depth:
-        pl.loop(depth, count)(lambda k: step(k, reuse=True))
     for k in range(count - depth, count):
         leave(k).wait()
 
@@ -315,15 +269,15 @@
     rows, units = saved_hidden.shape[1:]
     depth = D * E * CAP
     width = cols * T // D
-    tile, strip = 512, 1024
+    tile, strip = 256, 1024
     if (
-        D != 2 or T % D or cols % (128 * D) or units % (8 * tile) or width % strip
+        D != 2 or T % D or cols % (128 * D) or units % (16 * tile) or width % strip
         or rows != E * CAP or tokens % 128
     ):
         return plain(grad_out, expert_ids, route_gates, saved_hidden)
     q = T // D
     hidden = saved_hidden[0]
-    share = units // 8
+    share = units // 16
     ahead, stop = EARLY * share, INSIDE * share
     later, at = [], stop
     for part in LATER:
@@ -331,7 +285,7 @@
         at += part * share
     later = tuple(later)
     vmem = pl.BlockSpec(memory_space=pltpu.VMEM)
-    hbm = pl.BlockSpec(memory_space=pl.ANY)
+    hbm = pl.BlockSpec(memory_space=pltpu.HBM)
     dma = pltpu.SemaphoreType.DMA
     bf16 = jnp.bfloat16
     swap = [(0, 1), (1, 0)]
@@ -344,36 +298,36 @@
             *(jax.ShapeDtypeStruct((rows, size), bf16) for _, size in later),
         ),
         in_specs=[vmem, vmem, vmem, hbm],
-        out_specs=(vmem, hbm, *(hbm for _ in later)),
+        out_specs=(vmem, vmem, *(vmem for _ in later)),
         scratch_shapes=[
             pltpu.VMEM((E * CAP, cols), bf16),
-            pltpu.VMEM((rows, units - stop), bf16),
-            dma((len(later),)), dma((len(later),)),
+            dma((len(later),)),
             dma, dma,
             dma((E, D)), dma((D, E)),
             dma((D - 1, D, E)), dma((D - 1, D, E)),
             dma((q - 1, D, D, E)), dma((q - 1, D, D, E)),
         ],
         cost_estimate=pl.CostEstimate(flops=2 * 10**10, bytes_accessed=2**22, transcendentals=0),
-        compiler_params=pltpu.CompilerParams(has_side_effects=True, collective_id=0),
+        compiler_params=pltpu.CompilerParams(has_side_effects=True, collective_id=0, vmem_limit_bytes=16 * 2**20),
     )(expert_ids.T, route_gates.T, grad_out, hidden)
-    arrived = [lax.ppermute(part, "dp", swap) for part in parts]
+    arrived = []
+    for part in parts:
+        arrived.append(lax.ppermute(part, "dp", swap))
 
     def run(base, others, out):
         spans = tuple(o.shape[1] for o in others)
         count = sum(spans) // tile
-        slots = min(4, count)
+        slots = min(6, count)
         return pl.pallas_call(
             functools.partial(product, base, spans, tile, strip, slots),
             out_shape=jax.ShapeDtypeStruct((units, width), bf16),
-            in_specs=[hbm] * (len(others) + 2 + len(out)),
+            in_specs=[vmem, *(vmem for _ in others), vmem, *(hbm for _ in out)],
             out_specs=hbm,
             scratch_shapes=[
-                pltpu.VMEM((count, 2 * rows, tile), bf16),
-                pltpu.VMEM((depth, width), bf16),
                 pltpu.VMEM((slots, tile, width), bf16),
-                dma((count, 2)), dma((width // strip,)), dma((slots,)),
+                dma((slots,)),
             ],
+            compiler_params=pltpu.CompilerParams(vmem_limit_bytes=24 * 2**20),
             input_output_aliases={len(others) + 2: 0} if out else {},
             cost_estimate=pl.CostEstimate(
                 flops=2 * depth * width * count * tile,

time: 57.3 us -> 47.2 us (0.82)
  Pallas kernels: 43.8 us -> 32.6 us
  local copies, waits for them, and re-layouts: 3.55 us -> 4.49 us
    pallas_call x4 -> x3, Pallas kernels: 21.5 us -> 11.8 us  [run(): pl.pallas_call(functools.partial(product, base, spans, tile, strip, slots...]
    pallas_call x1, Pallas kernels: 22.3 us -> 20.8 us  [local(): pl.pallas_call(functools.partial(exchange, D, E, T, ahead, stop, later),...]
    unnamed x8 -> x10, local copies, waits for them, and re-layouts: 2.64 us -> 3.58 us
    ppermute x3 -> x2, waiting for transfers between devices: 4.16 us -> 4.53 us  [local(): arrived.append(lax.ppermute(part, 'dp', swap))]
    ppermute x3 -> x2, starting transfers between devices: 2.17 us -> 2.09 us  [local(): arrived.append(lax.ppermute(part, 'dp', swap))]
  transfers between devices with their start and end apart: 4 -> 3, of which waited for: 1 -> 1; matrix products, arithmetic and copies ran while one was open for 0% -> 0% of each run, Pallas kernels for 69% -> 64%
where the time goes in v3:
time: 47.2 us; the launch traced here: 46.8 us
  Pallas kernels  32.6 us (69%)
  starting transfers between devices  5.15 us (11%)
  waiting for transfers between devices  4.53 us (10%)
  local copies, waits for them, and re-layouts  4.49 us (10%)
    pallas_call x1, Pallas kernels, local(): pl.pallas_call(functools.partial(exchange, D, E, T, ahead, stop, later),...  20.8 us
    pallas_call x3, Pallas kernels, run(): pl.pallas_call(functools.partial(product, base, spans, tile, strip, slots...  11.8 us
    ppermute x2, waiting for transfers between devices, local(): arrived.append(lax.ppermute(part, 'dp', swap))  4.53 us
    unnamed x10, local copies, waits for them, and re-layouts  3.58 us
    ppermute x1, starting transfers between devices, local(): first = lax.ppermute(hidden[:, :ahead], 'dp', swap)  3.06 us
    ppermute x2, starting transfers between devices, local(): arrived.append(lax.ppermute(part, 'dp', swap))  2.09 us
  transfers between devices with their start and end apart: 3, of which 1 were waited for; matrix products, arithmetic and copies ran while one was open for 0% of the time, Pallas kernels for 64%

profile of v3, /device:TPU:0, one launch (start us, length us, event | category | flops | bytes accessed | tf_op | source)
XLA Modules:
  0.0 46.8 jit_solution(6050785070730986073)
XLA Ops:
  0.0 0.9 %slice.4 = bf16[128,512]{1,0:T(8,128)(2,1)S(1)} slice(bf16[128,4096]{1,0:T(8,128)(2,1)} %bitcast.4), slice={[0:128], [0:512]} | slice | bytes 262144 | tf_op jit(solution)/shard_map/slice | solution.py:292
  0.9 3.1 %collective-permute-start.2 = (bf16[128,512]{1,0:T(8,128)(2,1)S(1)}, bf16[128,512]{1,0:T(8,128)(2,1)S(1)}, u32[]{:S(2)}, u32[]{:S(2)}) collective-permute-start(bf16[128,512]{1,0:T(8,128)(2,1)S(1)} %slice.4), channel_id=1, source_target_pairs={{0,16},{16,0},{1,17},{17,1},{2,18},{18,2},{3,19},{19,3},{4,20},{20... | collective-permute-start | bytes 393224 | tf_op jit(solution)/shard_map/ppermute | solution.py:292
  4.0 0.0 copy-start
  4.0 1.2 %copy-done = bf16[1,128,4096]{2,1,0:T(8,128)(2,1)S(1)} copy-done((bf16[1,128,4096]{2,1,0:T(8,128)(2,1)S(1)}, bf16[1,128,4096]{2,1,0:T(8,128)(2,1)}, u32[]{:S(2)}) %copy-start) | copy-done | bytes 1048600
  5.2 0.0 copy-start.2
  5.2 1.0 %copy-done.2 = bf16[128,1536]{1,0:T(8,128)(2,1)S(1)} copy-done((bf16[128,1536]{1,0:T(8,128)(2,1)S(1)}, bf16[128,1536]{1,0:T(8,128)(2,1)}, u32[]{:S(2)}) %copy-start.2) | copy-done | bytes 393240
  6.2 0.0 copy-start.3
  6.2 0.7 %copy-done.3 = s32[128,2]{0,1:T(2,128)S(1)} copy-done((s32[128,2]{0,1:T(2,128)S(1)}, s32[128,2]{0,1:T(2,128)}, u32[]{:S(2)}) %copy-start.3) | copy-done | bytes 1048
  6.9 0.0 copy-start.4
  6.9 0.7 %copy-done.4 = f32[128,2]{0,1:T(2,128)S(1)} copy-done((f32[128,2]{0,1:T(2,128)S(1)}, f32[128,2]{0,1:T(2,128)}, u32[]{:S(2)}) %copy-start.4) | copy-done | bytes 1048
  7.6 0.0 copy-start.1
  7.6 20.8 %shard_map.46 = (bf16[256,3072]{1,0:T(8,128)(2,1)S(1)}, bf16[128,1792]{1,0:T(8,128)(2,1)S(1)}, bf16[128,1024]{1,0:T(8,128)(2,1)S(1)}, bf16[128,768]{1,0:T(8,128)(2,1)S(1)}) custom-call(s32[2,128]{1,0:T(2,128)S(1)} %bitcast.9, f32[2,128]{1,0:T(2,128)S(1)} %bitcast.10, bf16[128,1536]{1,0:T(8,128)(2,1)S(1)} %copy-done.2, bf16[128,4096]{1,0:T(8,128)(2,1)S(1)} %bitcast.5), custom_call_target="tpu_custom_call" | custom-call | flops 20000000000 | bytes 4194304 | tf_op jit(solution)/shard_map/pallas_call | solution.py:293
  28.3 0.6 %collective-permute-start = (bf16[128,768]{1,0:T(8,128)(2,1)S(1)}, bf16[128,768]{1,0:T(8,128)(2,1)S(1)}, u32[]{:S(2)}, u32[]{:S(2)}) collective-permute-start(bf16[128,768]{1,0:T(8,128)(2,1)S(1)} %get-tuple-element.9), channel_id=1, source_target_pairs={{0,16},{16,0},{1,17},{17,1},{2,18},{18,2},{3,19},{19,3},{4,20},{20... | collective-permute-start | bytes 589832 | tf_op jit(solution)/shard_map/ppermute | solution.py:315
  28.9 1.5 %collective-permute-start.1 = (bf16[128,1024]{1,0:T(8,128)(2,1)S(1)}, bf16[128,1024]{1,0:T(8,128)(2,1)S(1)}, u32[]{:S(2)}, u32[]{:S(2)}) collective-permute-start(bf16[128,1024]{1,0:T(8,128)(2,1)S(1)} %get-tuple-element.11), channel_id=1, source_target_pairs={{0,16},{16,0},{1,17},{17,1},{2,18},{18,2},{3,19},{19,3},{4,20},{20... | collective-permute-start | bytes 786440 | tf_op jit(solution)/shard_map/ppermute | solution.py:315
  30.4 0.0 collective-permute-done.2.refs_0_
  30.4 0.0 copy-done.1
  30.4 5.7 %shard_map.47.refs_2_ = bf16[4096,3072]{1,0:T(8,128)(2,1)} custom-call(bf16[128,4096]{1,0:T(8,128)(2,1)S(1)} %bitcast.6, bf16[128,512]{1,0:T(8,128)(2,1)S(1)} %collective-permute-done.2.refs_0_, bf16[128,1792]{1,0:T(8,128)(2,1)S(1)} %get-tuple-element.12.refs_1_, bf16[256,3072]{1,0:T(8,128)(2,1)S(1)} %get-tuple-element.10.refs_2_.refs_1_), custom_call_target="tpu_custom_call" | custom-call | flops 3623878656 | bytes 14155776 | tf_op jit(solution)/shard_map/pallas_call | solution.py:321
  36.2 4.5 %collective-permute-done.1.refs_0_ = bf16[128,1024]{1,0:T(8,128)(2,1)S(1)} collective-permute-done((bf16[128,1024]{1,0:T(8,128)(2,1)S(1)}, bf16[128,1024]{1,0:T(8,128)(2,1)S(1)}, u32[]{:S(2)}, u32[]{:S(2)}) %collective-permute-start.1) | collective-permute-done | bytes 262176 | tf_op jit(solution)/shard_map/ppermute | solution.py:315
  40.7 3.3 %shard_map.48.refs_2_ = bf16[4096,3072]{1,0:T(8,128)(2,1)} custom-call(bf16[128,4096]{1,0:T(8,128)(2,1)S(1)} %bitcast.7, bf16[128,1024]{1,0:T(8,128)(2,1)S(1)} %collective-permute-done.1.refs_0_, bf16[256,3072]{1,0:T(8,128)(2,1)S(1)} %get-tuple-element.10.refs_2_.refs_1_, bf16[4096,3072]{1,0:T(8,128)(2,1)} %shard_map.47.refs_2_), custom_call_target="tpu_custom_call", output_to_operand_aliasing={{}: (3, {})} | custom-call | flops 1610612736 | bytes 6291456 | tf_op jit(solution)/shard_map/pallas_call | solution.py:321
  44.0 0.0 collective-permute-done.refs_0_
  44.0 2.8 %shard_map.49 = bf16[4096,3072]{1,0:T(8,128)(2,1)} custom-call(bf16[128,4096]{1,0:T(8,128)(2,1)S(1)} %bitcast.8, bf16[128,768]{1,0:T(8,128)(2,1)S(1)} %collective-permute-done.refs_0_, bf16[256,3072]{1,0:T(8,128)(2,1)S(1)} %get-tuple-element.10.refs_2_.refs_1_, bf16[4096,3072]{1,0:T(8,128)(2,1)} %shard_map.48.refs_2_), custom_call_target="tpu_custom_call", output_to_operand_aliasing={{}: (3, {})} | custom-call | flops 1207959552 | bytes 4718592 | tf_op jit(solution)/shard_map/pallas_call | solution.py:321
Async XLA Ops:
  0.9 29.5 %collective-permute-start.2 = (bf16[128,512]{1,0:T(8,128)(2,1)S(1)}, bf16[128,512]{1,0:T(8,128)(2,1)S(1)}, u32[]{:S(2)}, u32[]{:S(2)}) collective-permute-start(bf16[128,512]{1,0:T(8,128)(2,1)S(1)} %slice.4), channel_id=1, source_target_pairs={{0,16},{16,0},{1,17},{17,1},{2,18},{18,2},{3,19},{19,3},{4,20},{20... | collective-permute-start | bytes 393224 | tf_op jit(solution)/shard_map/ppermute | solution.py:292
  4.0 1.2 %copy-start = (bf16[1,128,4096]{2,1,0:T(8,128)(2,1)S(1)}, bf16[1,128,4096]{2,1,0:T(8,128)(2,1)}, u32[]{:S(2)}) copy-start(bf16[1,128,4096]{2,1,0:T(8,128)(2,1)} %param.7) | copy-start | bytes 3145732
  5.2 1.0 %copy-start.2 = (bf16[128,1536]{1,0:T(8,128)(2,1)S(1)}, bf16[128,1536]{1,0:T(8,128)(2,1)}, u32[]{:S(2)}) copy-start(bf16[128,1536]{1,0:T(8,128)(2,1)} %grad_ref.1) | copy-start | bytes 1179652
  6.2 0.7 %copy-start.3 = (s32[128,2]{0,1:T(2,128)S(1)}, s32[128,2]{0,1:T(2,128)}, u32[]{:S(2)}) copy-start(s32[128,2]{0,1:T(2,128)} %param.5) | copy-start | bytes 3076
  6.9 0.7 %copy-start.4 = (f32[128,2]{0,1:T(2,128)S(1)}, f32[128,2]{0,1:T(2,128)}, u32[]{:S(2)}) copy-start(f32[128,2]{0,1:T(2,128)} %param.6) | copy-start | bytes 3076
  7.6 22.9 %copy-start.1 = (bf16[1,128,4096]{2,1,0:T(8,128)(2,1)S(1)}, bf16[1,128,4096]{2,1,0:T(8,128)(2,1)}, u32[]{:S(2)}) copy-start(bf16[1,128,4096]{2,1,0:T(8,128)(2,1)} %param.7) | copy-start | bytes 3145732
  28.3 15.7 %collective-permute-start = (bf16[128,768]{1,0:T(8,128)(2,1)S(1)}, bf16[128,768]{1,0:T(8,128)(2,1)S(1)}, u32[]{:S(2)}, u32[]{:S(2)}) collective-permute-start(bf16[128,768]{1,0:T(8,128)(2,1)S(1)} %get-tuple-element.9), channel_id=1, source_target_pairs={{0,16},{16,0},{1,17},{17,1},{2,18},{18,2},{3,19},{19,3},{4,20},{20... | collective-permute-start | bytes 589832 | tf_op jit(solution)/shard_map/ppermute | solution.py:315
  28.9 11.8 %collective-permute-start.1 = (bf16[128,1024]{1,0:T(8,128)(2,1)S(1)}, bf16[128,1024]{1,0:T(8,128)(2,1)S(1)}, u32[]{:S(2)}, u32[]{:S(2)}) collective-permute-start(bf16[128,1024]{1,0:T(8,128)(2,1)S(1)} %get-tuple-element.11), channel_id=1, source_target_pairs={{0,16},{16,0},{1,17},{17,1},{2,18},{18,2},{3,19},{19,3},{4,20},{20... | collective-permute-start | bytes 786440 | tf_op jit(solution)/shard_map/ppermute | solution.py:315

commit v4 on v3

--- a/solution.py
+++ b/solution.py
@@ -12,7 +12,7 @@
 CAP = 32
 MESH = pl.DeviceIdType.MESH
 TN = (((0,), (0,)), ((), ()))
-EARLY, INSIDE, LATER = 2, 9, (4, 3)
+EARLY, INSIDE, LATER = 0, 9, (4, 3)
 
 
 def slot_table(expert_ids, route_gates, expert_count):
@@ -76,11 +76,15 @@
     return (picked * slot_gate).astype(jnp.bfloat16)
 
 
+def flip(e, j):
+    return sum(((e // b + j // b) % 2) * b for b in (1, 2, 4, 8, 16))
+
+
 def exchange(
-    D, E, T, lo, hi, later, ids_ref, gates_ref, grad_ref, hidden_ref, g_ref, other_ref, *rest
+    D, E, T, lo, hi, later, ids_hbm, gates_hbm, grad_hbm, hidden_ref, g_ref, other_ref, *rest
 ):
     parts = rest[:len(later)]
-    (slots, p_in, h_send, h_recv, s1, r1, s2, r2, s3, r3) = rest[len(later):]
+    (ids_ref, gates_ref, grad_ref, loads, slots, p_in, h_send, h_recv, s1, r1, s2, r2, s3, r3) = rest[len(later):]
     d, e, t = lax.axis_index("dp"), lax.axis_index("expert"), lax.axis_index("tensor")
     q = T // D
     x, c = t // q, t % q
@@ -101,6 +105,14 @@
         at, size = later[i]
         return pltpu.make_async_copy(hidden_ref.at[:, pl.ds(at, size)], parts[i], p_in.at[i])
 
+    inputs = [
+        pltpu.make_async_copy(source, target, loads.at[i])
+        for i, (source, target) in enumerate(
+            ((ids_hbm, ids_ref), (gates_hbm, gates_ref), (grad_hbm, grad_ref))
+        )
+    ]
+    for copy in inputs:
+        copy.start()
     barrier = pltpu.get_barrier_semaphore()
 
     def greet(to):
@@ -120,6 +132,8 @@
                 greet(to)
     for i in range(len(later)):
         stage(i).start()
+    for copy in inputs:
+        copy.wait()
     slots[...] = slot_rows(ids_ref[...], gates_ref[...], grad_ref[...], E)
     pl.semaphore_wait(barrier, 2 * (D - 1) + q - 1 + D * E - jnp.where(x == d, 1, 0))
 
@@ -130,12 +144,12 @@
         ]
 
     def first(j, m):
-        e2, x2 = (e + j) % E, (x + m) % D
+        e2, x2 = flip(e, j), (x + m) % D
         r = (d - x + D) % D
         src = slots.at[
             pl.ds(pl.multiple_of(e2 * CAP, CAP), CAP), pl.ds(pl.multiple_of(x2 * W, 128), W)
         ]
-        return src, place(r, e, x2, c), r1.at[r, (E - j) % E], (x, e2, x2 * q + c)
+        return src, place(r, e, x2, c), r1.at[r, j], (x, e2, x2 * q + c)
 
     def first_remote(j, m):
         src, dst, sem, to = first(j, m)
@@ -150,7 +164,7 @@
         ]
         return pltpu.make_async_copy(src, place(0, e, x, c), r1.at[0, 0])
 
-    order = sorted(range(E), key=lambda j: -min(j, E - j))
+    order = [0, 1, 2, 3]
     for j in order:
         for m in range(D):
             if j == 0 and m == 0:
@@ -162,21 +176,21 @@
     hidden_copy().start()
 
     def along(n, r, k):
-        here = place(r, (e + k) % E, x, c)
+        here = place(r, flip(e, k), x, c)
         return pltpu.make_async_remote_copy(
             src_ref=here, dst_ref=here, send_sem=s2.at[n - 1, r, k], recv_sem=r2.at[D - n - 1, r, k],
             device_id=(d, e, ((x + n) % D) * q + c), device_id_type=MESH,
         )
 
     def along_arrived(n, r, k):
-        here = place(r, (e + k) % E, (x + n) % D, c)
+        here = place(r, flip(e, k), (x + n) % D, c)
         return pltpu.make_async_remote_copy(
             src_ref=here, dst_ref=here, send_sem=s2.at[n - 1, r, k], recv_sem=r2.at[n - 1, r, k],
             device_id=(d, e, ((x + n) % D) * q + c), device_id_type=MESH,
         )
 
     def across(p, n, r, k):
-        here = place(r, (e + k) % E, (x + n) % D, c)
+        here = place(r, flip(e, k), (x + n) % D, c)
         return pltpu.make_async_remote_copy(
             src_ref=here, dst_ref=here, send_sem=s3.at[p - 1, n, r, k],
             recv_sem=r3.at[q - p - 1, n, r, k],
@@ -184,7 +198,7 @@
         )
 
     def across_arrived(p, n, r, k):
-        here = place(r, (e + k) % E, (x + n) % D, (c + p) % q)
+        here = place(r, flip(e, k), (x + n) % D, (c + p) % q)
         return pltpu.make_async_remote_copy(
             src_ref=here, dst_ref=here, send_sem=s3.at[p - 1, n, r, k],
             recv_sem=r3.at[p - 1, n, r, k],
@@ -192,13 +206,13 @@
         )
 
     def first_arrived(r, k):
-        here = place(r, (e + k) % E, x, c)
+        here = place(r, flip(e, k), x, c)
         return pltpu.make_async_remote_copy(
             src_ref=here, dst_ref=here, send_sem=s1.at[0, 0], recv_sem=r1.at[r, k],
-            device_id=((d + r) % D, (e + k) % E, d * q + c), device_id_type=MESH,
-        )
-
-    blocks = [(r, k) for k in reversed(order) for r in range(D)]
+            device_id=((d + r) % D, flip(e, k), d * q + c), device_id_type=MESH,
+        )
+
+    blocks = [(r, k) for k in range(E) for r in range(D)]
     for r, k in blocks:
         if r == 0 and k == 0:
             pl.when(x == d)(lambda: first_local().wait())
@@ -244,23 +258,28 @@
     count = len(tiles)
     depth = min(slots, count)
 
-    def leave(k):
+    starts = range(0, width, strip)
+
+    def leave(k, i):
         return pltpu.make_async_copy(
-            ob.at[k % depth], o_ref.at[pl.ds(base + k * tile, tile), :], os.at[k % depth]
+            ob.at[k % depth, :, pl.ds(starts[i], strip)],
+            o_ref.at[pl.ds(base + k * tile, tile), pl.ds(starts[i], strip)],
+            os.at[k % depth, i],
         )
 
     for k, (other, at) in enumerate(tiles):
-        if k >= depth:
-            leave(k - depth).wait()
         mine = own_ref[:, base + k * tile:base + (k + 1) * tile]
         hidden = jnp.concatenate([mine, other[:, at:at + tile]], axis=0)
-        for lo in range(0, width, strip):
+        for i, lo in enumerate(starts):
+            if k >= depth:
+                leave(k - depth, i).wait()
             ob[k % depth, :, lo:lo + strip] = lax.dot_general(
                 hidden, g_ref[:, lo:lo + strip], TN, preferred_element_type=jnp.float32
             ).astype(ob.dtype)
-        leave(k).start()
+            leave(k, i).start()
     for k in range(count - depth, count):
-        leave(k).wait()
+        for i in range(len(starts)):
+            leave(k, i).wait()
 
 
 def local(grad_out, expert_ids, route_gates, saved_hidden):
@@ -271,7 +290,7 @@
     width = cols * T // D
     tile, strip = 256, 1024
     if (
-        D != 2 or T % D or cols % (128 * D) or units % (16 * tile) or width % strip
+        D != 2 or E & (E - 1) or E > 32 or T % D or cols % (128 * D) or units % (16 * tile) or width % strip
         or rows != E * CAP or tokens % 128
     ):
         return plain(grad_out, expert_ids, route_gates, saved_hidden)
@@ -289,17 +308,20 @@
     dma = pltpu.SemaphoreType.DMA
     bf16 = jnp.bfloat16
     swap = [(0, 1), (1, 0)]
-    first = lax.ppermute(hidden[:, :ahead], "dp", swap)
     g, other, *parts = pl.pallas_call(
         functools.partial(exchange, D, E, T, ahead, stop, later),
         out_shape=(
-            jax.ShapeDtypeStruct((depth, width), bf16),
-            jax.ShapeDtypeStruct((rows, stop - ahead), bf16),
-            *(jax.ShapeDtypeStruct((rows, size), bf16) for _, size in later),
+            pltpu.VMEM((depth, width), bf16),
+            pltpu.VMEM((rows, stop - ahead), bf16),
+            *(pltpu.VMEM((rows, size), bf16) for _, size in later),
         ),
-        in_specs=[vmem, vmem, vmem, hbm],
+        in_specs=[hbm] * 4,
         out_specs=(vmem, vmem, *(vmem for _ in later)),
         scratch_shapes=[
+            pltpu.VMEM((TOP, tokens), jnp.int32),
+            pltpu.VMEM((TOP, tokens), jnp.float32),
+            pltpu.VMEM((tokens, cols), bf16),
+            dma((3,)),
             pltpu.VMEM((E * CAP, cols), bf16),
             dma((len(later),)),
             dma, dma,
@@ -308,8 +330,11 @@
             dma((q - 1, D, D, E)), dma((q - 1, D, D, E)),
         ],
         cost_estimate=pl.CostEstimate(flops=2 * 10**10, bytes_accessed=2**22, transcendentals=0),
-        compiler_params=pltpu.CompilerParams(has_side_effects=True, collective_id=0, vmem_limit_bytes=16 * 2**20),
-    )(expert_ids.T, route_gates.T, grad_out, hidden)
+        compiler_params=pltpu.CompilerParams(has_side_effects=True, collective_id=0, vmem_limit_bytes=16777216),
+    )(*(
+        pltpu.with_memory_space_constraint(a, pltpu.HBM)
+        for a in (expert_ids.T, route_gates.T, grad_out, hidden)
+    ))
     arrived = []
     for part in parts:
         arrived.append(lax.ppermute(part, "dp", swap))
@@ -325,7 +350,7 @@
             out_specs=hbm,
             scratch_shapes=[
                 pltpu.VMEM((slots, tile, width), bf16),
-                dma((slots,)),
+                dma((slots, width // strip)),
             ],
             compiler_params=pltpu.CompilerParams(vmem_limit_bytes=24 * 2**20),
             input_output_aliases={len(others) + 2: 0} if out else {},
@@ -336,7 +361,7 @@
             ),
         )(hidden, *others, g, *out)
 
-    out = run(0, (first, other), ())
+    out = run(0, (other,), ())
     for (at, _), part in zip(later, arrived):
         out = run(at, (part,), (out,))
     return out[None]

time: 47.2 us -> 43.3 us (0.917)
  Pallas kernels: 32.6 us -> 37.4 us
  local copies, waits for them, and re-layouts: 4.49 us -> 0.01 us
  starting transfers between devices: 5.15 us -> 2.09 us
  waiting for transfers between devices: 4.53 us -> 3.59 us
    pallas_call x1, Pallas kernels: 20.8 us -> 25.4 us  [local(): pl.pallas_call(functools.partial(exchange, D, E, T, ahead, stop, later),...]
    unnamed x10 -> x2, local copies, waits for them, and re-layouts: 3.58 us -> 0.01 us
    ppermute x1 -> x0, starting transfers between devices: 3.06 us -> none  [local(): first = lax.ppermute(hidden[:, :ahead], 'dp', swap)]
    ppermute x2, waiting for transfers between devices: 4.53 us -> 3.59 us  [local(): arrived.append(lax.ppermute(part, 'dp', swap))]
    slice x1 -> x0, local copies, waits for them, and re-layouts: 0.91 us -> none  [local(): first = lax.ppermute(hidden[:, :ahead], 'dp', swap)]
  transfers between devices with their start and end apart: 3 -> 2, of which waited for: 1 -> 1; matrix products, arithmetic and copies ran while one was open for 0% -> 0% of each run, Pallas kernels for 64% -> 22%
where the time goes in v4:
time: 43.3 us; the launch traced here: 43.2 us
  Pallas kernels  37.4 us (86%)
  waiting for transfers between devices  3.59 us (8%)
  starting transfers between devices  2.09 us (5%)
    pallas_call x1, Pallas kernels, local(): pl.pallas_call(functools.partial(exchange, D, E, T, ahead, stop, later),...  25.4 us
    pallas_call x3, Pallas kernels, run(): pl.pallas_call(functools.partial(product, base, spans, tile, strip, slots...  12.1 us
    ppermute x2, waiting for transfers between devices, local(): arrived.append(lax.ppermute(part, 'dp', swap))  3.59 us
    ppermute x2, starting transfers between devices, local(): arrived.append(lax.ppermute(part, 'dp', swap))  2.09 us
  transfers between devices with their start and end apart: 2, of which 1 were waited for; matrix products, arithmetic and copies ran while one was open for 0% of the time, Pallas kernels for 22%

profile of v4, /device:TPU:0, one launch (start us, length us, event | category | flops | bytes accessed | tf_op | source)
XLA Modules:
  0.0 43.2 jit_solution(12122732997970441749)
XLA Ops:
  0.0 0.0 copy-start
  0.0 25.4 %shard_map.46 = (bf16[256,3072]{1,0:T(8,128)(2,1)S(1)}, bf16[128,2304]{1,0:T(8,128)(2,1)S(1)}, bf16[128,1024]{1,0:T(8,128)(2,1)S(1)}, bf16[128,768]{1,0:T(8,128)(2,1)S(1)}) custom-call(s32[2,128]{1,0:T(2,128)} %bitcast.8, f32[2,128]{1,0:T(2,128)} %bitcast.9, bf16[128,1536]{1,0:T(8,128)(2,1)} %grad_hbm.1, bf16[128,4096]{1,0:T(8,128)(2,1)} %bitcast.4), custom_call_target="tpu_custom_call" | custom-call | flops 20000000000 | bytes 4194304 | tf_op jit(solution)/shard_map/pallas_call | solution.py:311
  25.4 0.9 %collective-permute-start = (bf16[128,768]{1,0:T(8,128)(2,1)S(1)}, bf16[128,768]{1,0:T(8,128)(2,1)S(1)}, u32[]{:S(2)}, u32[]{:S(2)}) collective-permute-start(bf16[128,768]{1,0:T(8,128)(2,1)S(1)} %get-tuple-element.9), channel_id=1, source_target_pairs={{0,16},{16,0},{1,17},{17,1},{2,18},{18,2},{3,19},{19,3},{4,20},{20... | collective-permute-start | bytes 589832 | tf_op jit(solution)/shard_map/ppermute | solution.py:340
  26.3 1.2 %collective-permute-start.1 = (bf16[128,1024]{1,0:T(8,128)(2,1)S(1)}, bf16[128,1024]{1,0:T(8,128)(2,1)S(1)}, u32[]{:S(2)}, u32[]{:S(2)}) collective-permute-start(bf16[128,1024]{1,0:T(8,128)(2,1)S(1)} %get-tuple-element.11), channel_id=1, source_target_pairs={{0,16},{16,0},{1,17},{17,1},{2,18},{18,2},{3,19},{19,3},{4,20},{20... | collective-permute-start | bytes 786440 | tf_op jit(solution)/shard_map/ppermute | solution.py:340
  27.5 0.0 copy-done
  27.5 6.4 %shard_map.47.refs_2_ = bf16[4096,3072]{1,0:T(8,128)(2,1)} custom-call(bf16[128,4096]{1,0:T(8,128)(2,1)S(1)} %bitcast.5, bf16[128,2304]{1,0:T(8,128)(2,1)S(1)} %get-tuple-element.12.refs_0_, bf16[256,3072]{1,0:T(8,128)(2,1)S(1)} %get-tuple-element.10.refs_1_), custom_call_target="tpu_custom_call" | custom-call | flops 3623878656 | bytes 14155776 | tf_op jit(solution)/shard_map/pallas_call | solution.py:346
  33.9 3.6 %collective-permute-done.1.refs_0_ = bf16[128,1024]{1,0:T(8,128)(2,1)S(1)} collective-permute-done((bf16[128,1024]{1,0:T(8,128)(2,1)S(1)}, bf16[128,1024]{1,0:T(8,128)(2,1)S(1)}, u32[]{:S(2)}, u32[]{:S(2)}) %collective-permute-start.1) | collective-permute-done | bytes 262176 | tf_op jit(solution)/shard_map/ppermute | solution.py:340
  37.5 3.1 %shard_map.48.refs_2_ = bf16[4096,3072]{1,0:T(8,128)(2,1)} custom-call(bf16[128,4096]{1,0:T(8,128)(2,1)S(1)} %bitcast.6, bf16[128,1024]{1,0:T(8,128)(2,1)S(1)} %collective-permute-done.1.refs_0_, bf16[256,3072]{1,0:T(8,128)(2,1)S(1)} %get-tuple-element.10.refs_1_, bf16[4096,3072]{1,0:T(8,128)(2,1)} %shard_map.47.refs_2_), custom_call_target="tpu_custom_call", output_to_operand_aliasing={{}: (3, {})} | custom-call | flops 1610612736 | bytes 6291456 | tf_op jit(solution)/shard_map/pallas_call | solution.py:346
  40.6 0.0 collective-permute-done.refs_0_
  40.6 2.6 %shard_map.49 = bf16[4096,3072]{1,0:T(8,128)(2,1)} custom-call(bf16[128,4096]{1,0:T(8,128)(2,1)S(1)} %bitcast.7, bf16[128,768]{1,0:T(8,128)(2,1)S(1)} %collective-permute-done.refs_0_, bf16[256,3072]{1,0:T(8,128)(2,1)S(1)} %get-tuple-element.10.refs_1_, bf16[4096,3072]{1,0:T(8,128)(2,1)} %shard_map.48.refs_2_), custom_call_target="tpu_custom_call", output_to_operand_aliasing={{}: (3, {})} | custom-call | flops 1207959552 | bytes 4718592 | tf_op jit(solution)/shard_map/pallas_call | solution.py:346
Async XLA Ops:
  0.0 27.5 %copy-start = (bf16[1,128,4096]{2,1,0:T(8,128)(2,1)S(1)}, bf16[1,128,4096]{2,1,0:T(8,128)(2,1)}, u32[]{:S(2)}) copy-start(bf16[1,128,4096]{2,1,0:T(8,128)(2,1)} %param.7) | copy-start | bytes 3145732
  25.4 15.2 %collective-permute-start = (bf16[128,768]{1,0:T(8,128)(2,1)S(1)}, bf16[128,768]{1,0:T(8,128)(2,1)S(1)}, u32[]{:S(2)}, u32[]{:S(2)}) collective-permute-start(bf16[128,768]{1,0:T(8,128)(2,1)S(1)} %get-tuple-element.9), channel_id=1, source_target_pairs={{0,16},{16,0},{1,17},{17,1},{2,18},{18,2},{3,19},{19,3},{4,20},{20... | collective-permute-start | bytes 589832 | tf_op jit(solution)/shard_map/ppermute | solution.py:340
  26.3 11.2 %collective-permute-start.1 = (bf16[128,1024]{1,0:T(8,128)(2,1)S(1)}, bf16[128,1024]{1,0:T(8,128)(2,1)S(1)}, u32[]{:S(2)}, u32[]{:S(2)}) collective-permute-start(bf16[128,1024]{1,0:T(8,128)(2,1)S(1)} %get-tuple-element.11), channel_id=1, source_target_pairs={{0,16},{16,0},{1,17},{17,1},{2,18},{18,2},{3,19},{19,3},{4,20},{20... | collective-permute-start | bytes 786440 | tf_op jit(solution)/shard_map/ppermute | solution.py:340

commit v5 on v4

--- a/solution.py
+++ b/solution.py
@@ -12,7 +12,7 @@
 CAP = 32
 MESH = pl.DeviceIdType.MESH
 TN = (((0,), (0,)), ((), ()))
-EARLY, INSIDE, LATER = 0, 9, (4, 3)
+EARLY, INSIDE, LATER = 4, 11, (5,)
 
 
 def slot_table(expert_ids, route_gates, expert_count):
@@ -84,7 +84,7 @@
     D, E, T, lo, hi, later, ids_hbm, gates_hbm, grad_hbm, hidden_ref, g_ref, other_ref, *rest
 ):
     parts = rest[:len(later)]
-    (ids_ref, gates_ref, grad_ref, loads, slots, p_in, h_send, h_recv, s1, r1, s2, r2, s3, r3) = rest[len(later):]
+    (ids_ref, gates_ref, grad_ref, near, loads, slots, p_in, h_send, h_recv, s1, r1, s2, r2, s3, r3) = rest[len(later):]
     d, e, t = lax.axis_index("dp"), lax.axis_index("expert"), lax.axis_index("tensor")
     q = T // D
     x, c = t // q, t % q
@@ -93,7 +93,7 @@
 
     def hidden_copy():
         return pltpu.make_async_remote_copy(
-            src_ref=hidden_ref.at[:, pl.ds(lo, hi - lo)],
+            src_ref=near,
             dst_ref=other_ref,
             send_sem=h_send,
             recv_sem=h_recv,
@@ -108,7 +108,10 @@
     inputs = [
         pltpu.make_async_copy(source, target, loads.at[i])
         for i, (source, target) in enumerate(
-            ((ids_hbm, ids_ref), (gates_hbm, gates_ref), (grad_hbm, grad_ref))
+            (
+                (ids_hbm, ids_ref), (gates_hbm, gates_ref), (grad_hbm, grad_ref),
+                (hidden_ref.at[:, pl.ds(lo, hi - lo)], near),
+            )
         )
     ]
     for copy in inputs:
@@ -132,7 +135,7 @@
                 greet(to)
     for i in range(len(later)):
         stage(i).start()
-    for copy in inputs:
+    for copy in inputs[:3]:
         copy.wait()
     slots[...] = slot_rows(ids_ref[...], gates_ref[...], grad_ref[...], E)
     pl.semaphore_wait(barrier, 2 * (D - 1) + q - 1 + D * E - jnp.where(x == d, 1, 0))
@@ -173,6 +176,7 @@
             else:
                 first_remote(j, m).start()
 
+    inputs[3].wait()
     hidden_copy().start()
 
     def along(n, r, k):
@@ -249,37 +253,40 @@
     hidden_copy().wait()
 
 
-def product(base, spans, tile, strip, slots, own_ref, *refs):
+def product(base, spans, tile, strip, own_ref, *refs):
     others = refs[:len(spans)]
     g_ref = refs[len(spans)]
     o_ref, ob, os = refs[-3:]
     width = g_ref.shape[1]
     tiles = [(o, at) for o, size in zip(others, spans) for at in range(0, size, tile)]
     count = len(tiles)
-    depth = min(slots, count)
 
     starts = range(0, width, strip)
-
-    def leave(k, i):
+    fine = 0 if count < 6 else count - 1
+    pieces = [(k, 0, width) for k in range(fine)]
+    pieces += [(k, lo, strip) for k in range(fine, count) for lo in starts]
+
+    def leave(i):
+        k, lo, size = pieces[i]
         return pltpu.make_async_copy(
-            ob.at[k % depth, :, pl.ds(starts[i], strip)],
-            o_ref.at[pl.ds(base + k * tile, tile), pl.ds(starts[i], strip)],
-            os.at[k % depth, i],
+            ob.at[k, :, pl.ds(lo, size)],
+            o_ref.at[pl.ds(base + k * tile, tile), pl.ds(lo, size)],
+            os.at[i],
         )
 
     for k, (other, at) in enumerate(tiles):
         mine = own_ref[:, base + k * tile:base + (k + 1) * tile]
         hidden = jnp.concatenate([mine, other[:, at:at + tile]], axis=0)
         for i, lo in enumerate(starts):
-            if k >= depth:
-                leave(k - depth, i).wait()
-            ob[k % depth, :, lo:lo + strip] = lax.dot_general(
+            ob[k, :, lo:lo + strip] = lax.dot_general(
                 hidden, g_ref[:, lo:lo + strip], TN, preferred_element_type=jnp.float32
             ).astype(ob.dtype)
-            leave(k, i).start()
-    for k in range(count - depth, count):
-        for i in range(len(starts)):
-            leave(k, i).wait()
+            if k >= fine:
+                leave(fine + (k - fine) * len(starts) + i).start()
+        if k < fine:
+            leave(k).start()
+    for i in range(len(pieces)):
+        leave(i).wait()
 
 
 def local(grad_out, expert_ids, route_gates, saved_hidden):
@@ -308,6 +315,7 @@
     dma = pltpu.SemaphoreType.DMA
     bf16 = jnp.bfloat16
     swap = [(0, 1), (1, 0)]
+    first = lax.ppermute(hidden[:, :ahead], "dp", swap)
     g, other, *parts = pl.pallas_call(
         functools.partial(exchange, D, E, T, ahead, stop, later),
         out_shape=(
@@ -321,7 +329,8 @@
             pltpu.VMEM((TOP, tokens), jnp.int32),
             pltpu.VMEM((TOP, tokens), jnp.float32),
             pltpu.VMEM((tokens, cols), bf16),
-            dma((3,)),
+            pltpu.VMEM((rows, stop - ahead), bf16),
+            dma((4,)),
             pltpu.VMEM((E * CAP, cols), bf16),
             dma((len(later),)),
             dma, dma,
@@ -342,17 +351,16 @@
     def run(base, others, out):
         spans = tuple(o.shape[1] for o in others)
         count = sum(spans) // tile
-        slots = min(6, count)
         return pl.pallas_call(
-            functools.partial(product, base, spans, tile, strip, slots),
+            functools.partial(product, base, spans, tile, strip),
             out_shape=jax.ShapeDtypeStruct((units, width), bf16),
             in_specs=[vmem, *(vmem for _ in others), vmem, *(hbm for _ in out)],
             out_specs=hbm,
             scratch_shapes=[
-                pltpu.VMEM((slots, tile, width), bf16),
-                dma((slots, width // strip)),
+                pltpu.VMEM((count, tile, width), bf16),
+                dma((count + 6 * width // strip,)),
             ],
-            compiler_params=pltpu.CompilerParams(vmem_limit_bytes=24 * 2**20),
+            compiler_params=pltpu.CompilerParams(vmem_limit_bytes=30 * 2**20),
             input_output_aliases={len(others) + 2: 0} if out else {},
             cost_estimate=pl.CostEstimate(
                 flops=2 * depth * width * count * tile,
@@ -361,7 +369,7 @@
             ),
         )(hidden, *others, g, *out)
 
-    out = run(0, (other,), ())
+    out = run(0, (first, other), ())
     for (at, _), part in zip(later, arrived):
         out = run(at, (part,), (out,))
     return out[None]

time: 43.3 us -> 38.4 us (0.89)
  Pallas kernels: 37.4 us -> 31.5 us
  starting transfers between devices: 2.09 us -> 4.87 us
  waiting for transfers between devices: 3.59 us -> 0.97 us
  local copies, waits for them, and re-layouts: 0.01 us -> 0.97 us
    pallas_call x1, Pallas kernels: 25.4 us -> 21 us  [local(): pl.pallas_call(functools.partial(exchange, D, E, T, ahead, stop, later),...]
    ppermute x0 -> x1, starting transfers between devices: none -> 3.06 us  [local(): first = lax.ppermute(hidden[:, :ahead], 'dp', swap)]
    ppermute x2 -> x1, waiting for transfers between devices: 3.59 us -> 0.96 us  [local(): arrived.append(lax.ppermute(part, 'dp', swap))]
    pallas_call x3 -> x2, Pallas kernels: 12.1 us -> 10.5 us  [run(): pl.pallas_call(functools.partial(product, base, spans, tile, strip), out_...]
    slice x0 -> x1, local copies, waits for them, and re-layouts: none -> 0.97 us  [local(): first = lax.ppermute(hidden[:, :ahead], 'dp', swap)]
    ppermute x2 -> x1, starting transfers between devices: 2.09 us -> 1.81 us  [local(): arrived.append(lax.ppermute(part, 'dp', swap))]
  transfers between devices with their start and end apart: 2 -> 2, of which waited for: 1 -> 1; matrix products, arithmetic and copies ran while one was open for 0% -> 0% of each run, Pallas kernels for 22% -> 73%
where the time goes in v5:
time: 38.4 us; the launch traced here: 38.3 us
  Pallas kernels  31.5 us (82%)
  starting transfers between devices  4.87 us (13%)
  local copies, waits for them, and re-layouts  0.97 us (3%)
  waiting for transfers between devices  0.97 us (3%)
    pallas_call x1, Pallas kernels, local(): pl.pallas_call(functools.partial(exchange, D, E, T, ahead, stop, later),...  21 us
    pallas_call x2, Pallas kernels, run(): pl.pallas_call(functools.partial(product, base, spans, tile, strip), out_...  10.5 us
    ppermute x1, starting transfers between devices, local(): first = lax.ppermute(hidden[:, :ahead], 'dp', swap)  3.06 us
    ppermute x1, starting transfers between devices, local(): arrived.append(lax.ppermute(part, 'dp', swap))  1.81 us
    slice x1, local copies, waits for them, and re-layouts, local(): first = lax.ppermute(hidden[:, :ahead], 'dp', swap)  0.97 us
    ppermute x1, waiting for transfers between devices, local(): arrived.append(lax.ppermute(part, 'dp', swap))  0.96 us
  transfers between devices with their start and end apart: 2, of which 1 were waited for; matrix products, arithmetic and copies ran while one was open for 0% of the time, Pallas kernels for 73%

profile of v5, /device:TPU:0, one launch (start us, length us, event | category | flops | bytes accessed | tf_op | source)
XLA Modules:
  0.0 38.3 jit_solution(3880306387991920554)
XLA Ops:
  0.0 1.0 %slice.4 = bf16[128,1024]{1,0:T(8,128)(2,1)S(1)} slice(bf16[128,4096]{1,0:T(8,128)(2,1)} %bitcast.4), slice={[0:128], [0:1024]} | slice | bytes 524288 | tf_op jit(solution)/shard_map/slice | solution.py:318
  1.0 3.1 %collective-permute-start.1 = (bf16[128,1024]{1,0:T(8,128)(2,1)S(1)}, bf16[128,1024]{1,0:T(8,128)(2,1)S(1)}, u32[]{:S(2)}, u32[]{:S(2)}) collective-permute-start(bf16[128,1024]{1,0:T(8,128)(2,1)S(1)} %slice.4), channel_id=1, source_target_pairs={{0,16},{16,0},{1,17},{17,1},{2,18},{18,2},{3,19},{19,3},{4,20},{20... | collective-permute-start | bytes 786440 | tf_op jit(solution)/shard_map/ppermute | solution.py:318
  4.0 0.0 copy-start
  4.0 21.0 %shard_map.46 = (bf16[256,3072]{1,0:T(8,128)(2,1)S(1)}, bf16[128,1792]{1,0:T(8,128)(2,1)S(1)}, bf16[128,1280]{1,0:T(8,128)(2,1)S(1)}) custom-call(s32[2,128]{1,0:T(2,128)} %bitcast.8, f32[2,128]{1,0:T(2,128)} %bitcast.9, bf16[128,1536]{1,0:T(8,128)(2,1)} %grad_hbm.1, bf16[128,4096]{1,0:T(8,128)(2,1)} %bitcast.5), custom_call_target="tpu_custom_call" | custom-call | flops 20000000000 | bytes 4194304 | tf_op jit(solution)/shard_map/pallas_call | solution.py:319
  25.0 1.8 %collective-permute-start = (bf16[128,1280]{1,0:T(8,128)(2,1)S(1)}, bf16[128,1280]{1,0:T(8,128)(2,1)S(1)}, u32[]{:S(2)}, u32[]{:S(2)}) collective-permute-start(bf16[128,1280]{1,0:T(8,128)(2,1)S(1)} %get-tuple-element.8), channel_id=1, source_target_pairs={{0,16},{16,0},{1,17},{17,1},{2,18},{18,2},{3,19},{19,3},{4,20},{20... | collective-permute-start | bytes 983048 | tf_op jit(solution)/shard_map/ppermute | solution.py:349
  26.8 0.0 collective-permute-done.1.refs_0_
  26.8 0.0 copy-done
  26.8 6.8 %shard_map.47.refs_2_ = bf16[4096,3072]{1,0:T(8,128)(2,1)} custom-call(bf16[128,4096]{1,0:T(8,128)(2,1)S(1)} %bitcast.6, bf16[128,1024]{1,0:T(8,128)(2,1)S(1)} %collective-permute-done.1.refs_0_, bf16[128,1792]{1,0:T(8,128)(2,1)S(1)} %get-tuple-element.10.refs_1_, bf16[256,3072]{1,0:T(8,128)(2,1)S(1)} %get-tuple-element.9.refs_2_.refs_1_), custom_call_target="tpu_custom_call" | custom-call | flops 4429185024 | bytes 17301504 | tf_op jit(solution)/shard_map/pallas_call | solution.py:354
  33.7 1.0 %collective-permute-done.refs_0_ = bf16[128,1280]{1,0:T(8,128)(2,1)S(1)} collective-permute-done((bf16[128,1280]{1,0:T(8,128)(2,1)S(1)}, bf16[128,1280]{1,0:T(8,128)(2,1)S(1)}, u32[]{:S(2)}, u32[]{:S(2)}) %collective-permute-start) | collective-permute-done | bytes 327712 | tf_op jit(solution)/shard_map/ppermute | solution.py:349
  34.6 3.6 %shard_map.48 = bf16[4096,3072]{1,0:T(8,128)(2,1)} custom-call(bf16[128,4096]{1,0:T(8,128)(2,1)S(1)} %bitcast.7, bf16[128,1280]{1,0:T(8,128)(2,1)S(1)} %collective-permute-done.refs_0_, bf16[256,3072]{1,0:T(8,128)(2,1)S(1)} %get-tuple-element.9.refs_2_.refs_1_, bf16[4096,3072]{1,0:T(8,128)(2,1)} %shard_map.47.refs_2_), custom_call_target="tpu_custom_call", output_to_operand_aliasing={{}: (3, {})} | custom-call | flops 2013265920 | bytes 7864320 | tf_op jit(solution)/shard_map/pallas_call | solution.py:354
Async XLA Ops:
  1.0 25.9 %collective-permute-start.1 = (bf16[128,1024]{1,0:T(8,128)(2,1)S(1)}, bf16[128,1024]{1,0:T(8,128)(2,1)S(1)}, u32[]{:S(2)}, u32[]{:S(2)}) collective-permute-start(bf16[128,1024]{1,0:T(8,128)(2,1)S(1)} %slice.4), channel_id=1, source_target_pairs={{0,16},{16,0},{1,17},{17,1},{2,18},{18,2},{3,19},{19,3},{4,20},{20... | collective-permute-start | bytes 786440 | tf_op jit(solution)/shard_map/ppermute | solution.py:318
  4.0 22.8 %copy-start = (bf16[1,128,4096]{2,1,0:T(8,128)(2,1)S(1)}, bf16[1,128,4096]{2,1,0:T(8,128)(2,1)}, u32[]{:S(2)}) copy-start(bf16[1,128,4096]{2,1,0:T(8,128)(2,1)} %param.7) | copy-start | bytes 3145732
  25.0 9.6 %collective-permute-start = (bf16[128,1280]{1,0:T(8,128)(2,1)S(1)}, bf16[128,1280]{1,0:T(8,128)(2,1)S(1)}, u32[]{:S(2)}, u32[]{:S(2)}) collective-permute-start(bf16[128,1280]{1,0:T(8,128)(2,1)S(1)} %get-tuple-element.8), channel_id=1, source_target_pairs={{0,16},{16,0},{1,17},{17,1},{2,18},{18,2},{3,19},{19,3},{4,20},{20... | collective-permute-start | bytes 983048 | tf_op jit(solution)/shard_map/ppermute | solution.py:349

commit v6 on v5

--- a/solution.py
+++ b/solution.py
@@ -12,7 +12,7 @@
 CAP = 32
 MESH = pl.DeviceIdType.MESH
 TN = (((0,), (0,)), ((), ()))
-EARLY, INSIDE, LATER = 4, 11, (5,)
+EARLY, INSIDE, LATER, READY = 4, 11, (3, 2), 2
 
 
 def slot_table(expert_ids, route_gates, expert_count):
@@ -80,23 +80,38 @@
     return sum(((e // b + j // b) % 2) * b for b in (1, 2, 4, 8, 16))
 
 
+def multiply(mine, other, g_ref, out_ref, strip, after=lambda lo: None):
+    hidden = jnp.concatenate([mine, other], axis=0)
+    for lo in range(0, g_ref.shape[1], strip):
+        out_ref[:, lo:lo + strip] = lax.dot_general(
+            hidden, g_ref[:, lo:lo + strip], TN, preferred_element_type=jnp.float32
+        ).astype(out_ref.dtype)
+        after(lo)
+
+
 def exchange(
-    D, E, T, lo, hi, later, ids_hbm, gates_hbm, grad_hbm, hidden_ref, g_ref, other_ref, *rest
+    D, E, T, lo, hi, done, tile, strip, later, ids_hbm, gates_hbm, grad_hbm, hidden_ref, g_ref, other_ref, pre_ref,
+    *rest
 ):
     parts = rest[:len(later)]
-    (ids_ref, gates_ref, grad_ref, near, loads, slots, p_in, h_send, h_recv, s1, r1, s2, r2, s3, r3) = rest[len(later):]
+    (
+        ids_ref, gates_ref, grad_ref, near, loads, slots, p_in, h_send, h_recv, s1, r1, s2, r2, s3, r3
+    ) = rest[len(later):]
     d, e, t = lax.axis_index("dp"), lax.axis_index("expert"), lax.axis_index("tensor")
     q = T // D
     x, c = t // q, t % q
     cols = grad_ref.shape[1]
     W = cols // D
 
-    def hidden_copy():
-        return pltpu.make_async_remote_copy(
-            src_ref=near,
-            dst_ref=other_ref,
-            send_sem=h_send,
-            recv_sem=h_recv,
+    cuts = (0, done, hi - lo)
+
+    def hidden_copy(i):
+        part = pl.ds(cuts[i], cuts[i + 1] - cuts[i])
+        return pltpu.make_async_remote_copy(
+            src_ref=near.at[:, part],
+            dst_ref=other_ref.at[:, part],
+            send_sem=h_send.at[i],
+            recv_sem=h_recv.at[i],
             device_id=((d + 1) % D, e, t),
             device_id_type=MESH,
         )
@@ -167,7 +182,7 @@
         ]
         return pltpu.make_async_copy(src, place(0, e, x, c), r1.at[0, 0])
 
-    order = [0, 1, 2, 3]
+    order = range(E)
     for j in order:
         for m in range(D):
             if j == 0 and m == 0:
@@ -177,7 +192,8 @@
                 first_remote(j, m).start()
 
     inputs[3].wait()
-    hidden_copy().start()
+    for i in range(2):
+        hidden_copy(i).start()
 
     def along(n, r, k):
         here = place(r, flip(e, k), x, c)
@@ -236,6 +252,9 @@
         for p in range(1, q):
             for n in range(D):
                 across_arrived(p, n, r, k).wait_recv()
+    hidden_copy(0).wait_recv()
+    for at in range(0, done, tile):
+        multiply(near[:, at:at + tile], other_ref[:, at:at + tile], g_ref, pre_ref.at[pl.ds(at, tile)], strip)
     for j in order:
         for m in range(D):
             if j == 0 and m == 0:
@@ -250,43 +269,38 @@
                 across(p, n, r, k).wait_send()
     for i in range(len(later)):
         stage(i).wait()
-    hidden_copy().wait()
-
-
-def product(base, spans, tile, strip, own_ref, *refs):
-    others = refs[:len(spans)]
-    g_ref = refs[len(spans)]
+    hidden_copy(0).wait_send()
+    hidden_copy(1).wait()
+
+
+def product(base, tiles, ready, tile, strip, own_ref, *refs):
     o_ref, ob, os = refs[-3:]
+    others = refs[:1 + max(i for _, i, _ in tiles)]
+    g_ref, *whole = refs[len(others):-3]
     width = g_ref.shape[1]
-    tiles = [(o, at) for o, size in zip(others, spans) for at in range(0, size, tile)]
     count = len(tiles)
-
-    starts = range(0, width, strip)
     fine = 0 if count < 6 else count - 1
-    pieces = [(k, 0, width) for k in range(fine)]
-    pieces += [(k, lo, strip) for k in range(fine, count) for lo in starts]
-
-    def leave(i):
-        k, lo, size = pieces[i]
-        return pltpu.make_async_copy(
-            ob.at[k, :, pl.ds(lo, size)],
-            o_ref.at[pl.ds(base + k * tile, tile), pl.ds(lo, size)],
-            os.at[i],
-        )
-
-    for k, (other, at) in enumerate(tiles):
-        mine = own_ref[:, base + k * tile:base + (k + 1) * tile]
-        hidden = jnp.concatenate([mine, other[:, at:at + tile]], axis=0)
-        for i, lo in enumerate(starts):
-            ob[k, :, lo:lo + strip] = lax.dot_general(
-                hidden, g_ref[:, lo:lo + strip], TN, preferred_element_type=jnp.float32
-            ).astype(ob.dtype)
-            if k >= fine:
-                leave(fine + (k - fine) * len(starts) + i).start()
+    sent = []
+
+    def send(source, row, lo, size):
+        copy = pltpu.make_async_copy(
+            source.at[:, pl.ds(lo, size)],
+            o_ref.at[pl.ds(base + row, source.shape[0]), pl.ds(lo, size)],
+            os.at[len(sent)],
+        )
+        copy.start()
+        sent.append(copy)
+
+    if ready:
+        send(whole[0], ready, 0, width)
+    for k, (row, i, at) in enumerate(tiles):
+        mine = own_ref[:, base + row:base + row + tile]
+        after = lambda lo: send(ob.at[k], row, lo, strip) if k >= fine else None
+        multiply(mine, others[i][:, at:at + tile], g_ref, ob.at[k], strip, after)
         if k < fine:
-            leave(k).start()
-    for i in range(len(pieces)):
-        leave(i).wait()
+            send(ob.at[k], row, 0, width)
+    for copy in sent:
+        copy.wait()
 
 
 def local(grad_out, expert_ids, route_gates, saved_hidden):
@@ -305,6 +319,7 @@
     hidden = saved_hidden[0]
     share = units // 16
     ahead, stop = EARLY * share, INSIDE * share
+    done = READY * share
     later, at = [], stop
     for part in LATER:
         later.append((at, part * share))
@@ -316,15 +331,16 @@
     bf16 = jnp.bfloat16
     swap = [(0, 1), (1, 0)]
     first = lax.ppermute(hidden[:, :ahead], "dp", swap)
-    g, other, *parts = pl.pallas_call(
-        functools.partial(exchange, D, E, T, ahead, stop, later),
+    g, other, pre, *parts = pl.pallas_call(
+        functools.partial(exchange, D, E, T, ahead, stop, done, tile, strip, later),
         out_shape=(
             pltpu.VMEM((depth, width), bf16),
             pltpu.VMEM((rows, stop - ahead), bf16),
+            pltpu.VMEM((done, width), bf16),
             *(pltpu.VMEM((rows, size), bf16) for _, size in later),
         ),
         in_specs=[hbm] * 4,
-        out_specs=(vmem, vmem, *(vmem for _ in later)),
+        out_specs=(vmem, vmem, vmem, *(vmem for _ in later)),
         scratch_shapes=[
             pltpu.VMEM((TOP, tokens), jnp.int32),
             pltpu.VMEM((TOP, tokens), jnp.float32),
@@ -333,7 +349,7 @@
             dma((4,)),
             pltpu.VMEM((E * CAP, cols), bf16),
             dma((len(later),)),
-            dma, dma,
+            dma((2,)), dma((2,)),
             dma((E, D)), dma((D, E)),
             dma((D - 1, D, E)), dma((D - 1, D, E)),
             dma((q - 1, D, D, E)), dma((q - 1, D, D, E)),
@@ -348,30 +364,32 @@
     for part in parts:
         arrived.append(lax.ppermute(part, "dp", swap))
 
-    def run(base, others, out):
-        spans = tuple(o.shape[1] for o in others)
-        count = sum(spans) // tile
+    def run(base, tiles, others, ready, pre, out):
+        count = len(tiles)
+        operands = (hidden, *others, g, *pre)
         return pl.pallas_call(
-            functools.partial(product, base, spans, tile, strip),
+            functools.partial(product, base, tiles, ready, tile, strip),
             out_shape=jax.ShapeDtypeStruct((units, width), bf16),
-            in_specs=[vmem, *(vmem for _ in others), vmem, *(hbm for _ in out)],
+            in_specs=[*(vmem for _ in operands), *(hbm for _ in out)],
             out_specs=hbm,
             scratch_shapes=[
                 pltpu.VMEM((count, tile, width), bf16),
-                dma((count + 6 * width // strip,)),
+                dma((1 + count * (width // strip),)),
             ],
             compiler_params=pltpu.CompilerParams(vmem_limit_bytes=30 * 2**20),
-            input_output_aliases={len(others) + 2: 0} if out else {},
+            input_output_aliases={len(operands): 0} if out else {},
             cost_estimate=pl.CostEstimate(
                 flops=2 * depth * width * count * tile,
                 bytes_accessed=2 * width * count * tile,
                 transcendentals=0,
             ),
-        )(hidden, *others, g, *out)
-
-    out = run(0, (first, other), ())
-    for (at, _), part in zip(later, arrived):
-        out = run(at, (part,), (out,))
+        )(*operands, *out)
+
+    tiles = [(at, 0, at) for at in range(0, ahead, tile)]
+    tiles += [(at, 1, at - ahead) for at in range(ahead + done, stop, tile)]
+    out = run(0, tiles, (first, other), ahead, (pre,), ())
+    for (at, size), part in zip(later, arrived):
+        out = run(at, [(k, 0, k) for k in range(0, size, tile)], (part,), 0, (), (out,))
     return out[None]
 
 

time: 38.4 us -> 40.5 us (1.055)
  waiting for transfers between devices: 0.97 us -> 2.32 us
    ppermute x1 -> x2, waiting for transfers between devices: 0.96 us -> 2.32 us  [local(): arrived.append(lax.ppermute(part, 'dp', swap))]
    pallas_call x3 -> x4, Pallas kernels: 31.5 us -> 31.9 us  [the longest x1 21 us: local(): pl.pallas_call(functools.partial(exchange, D, E, T, ahead, stop, done, ti...]
    ppermute x1 -> x2, starting transfers between devices: 1.81 us -> 2.09 us  [local(): arrived.append(lax.ppermute(part, 'dp', swap))]
  transfers between devices with their start and end apart: 2 -> 3, of which waited for: 1 -> 1; matrix products, arithmetic and copies ran while one was open for 0% -> 0% of each run, Pallas kernels for 73% -> 74%
where the time goes in v6:
time: 40.5 us; the launch traced here: 40.3 us
  Pallas kernels  31.9 us (79%)
  starting transfers between devices  5.15 us (13%)
  waiting for transfers between devices  2.32 us (6%)
  local copies, waits for them, and re-layouts  0.97 us (2%)
    pallas_call x1, Pallas kernels, local(): pl.pallas_call(functools.partial(exchange, D, E, T, ahead, stop, done, ti...  21 us
    pallas_call x3, Pallas kernels, run(): pl.pallas_call(functools.partial(product, base, tiles, ready, tile, strip...  10.8 us
    ppermute x1, starting transfers between devices, local(): first = lax.ppermute(hidden[:, :ahead], 'dp', swap)  3.06 us
    ppermute x2, waiting for transfers between devices, local(): arrived.append(lax.ppermute(part, 'dp', swap))  2.32 us
    ppermute x2, starting transfers between devices, local(): arrived.append(lax.ppermute(part, 'dp', swap))  2.09 us
    slice x1, local copies, waits for them, and re-layouts, local(): first = lax.ppermute(hidden[:, :ahead], 'dp', swap)  0.97 us
  transfers between devices with their start and end apart: 3, of which 1 were waited for; matrix products, arithmetic and copies ran while one was open for 0% of the time, Pallas kernels for 74%

profile of v6, /device:TPU:0, one launch (start us, length us, event | category | flops | bytes accessed | tf_op | source)
XLA Modules:
  0.0 40.3 jit_solution(7247441693096554854)
XLA Ops:
  0.0 1.0 %slice.4 = bf16[128,1024]{1,0:T(8,128)(2,1)S(1)} slice(bf16[128,4096]{1,0:T(8,128)(2,1)} %bitcast.4), slice={[0:128], [0:1024]} | slice | bytes 524288 | tf_op jit(solution)/shard_map/slice | solution.py:333
  1.0 3.1 %collective-permute-start.2 = (bf16[128,1024]{1,0:T(8,128)(2,1)S(1)}, bf16[128,1024]{1,0:T(8,128)(2,1)S(1)}, u32[]{:S(2)}, u32[]{:S(2)}) collective-permute-start(bf16[128,1024]{1,0:T(8,128)(2,1)S(1)} %slice.4), channel_id=1, source_target_pairs={{0,16},{16,0},{1,17},{17,1},{2,18},{18,2},{3,19},{19,3},{4,20},{20... | collective-permute-start | bytes 786440 | tf_op jit(solution)/shard_map/ppermute | solution.py:333
  4.0 0.0 copy-start
  4.0 21.0 %shard_map.46 = (bf16[256,3072]{1,0:T(8,128)(2,1)S(1)}, bf16[128,1792]{1,0:T(8,128)(2,1)S(1)}, bf16[512,3072]{1,0:T(8,128)(2,1)S(1)}, bf16[128,768]{1,0:T(8,128)(2,1)S(1)}, bf16[128,512]{1,0:T(8,128)(2,1)S(1)}) custom-call(s32[2,128]{1,0:T(2,128)} %bitcast.9, f32[2,128]{1,0:T(2,128)} %bitcast.10, bf16[128,1536]{1,0:T(8,128)(2,1)} %grad_hbm.1, ...), custom_call_target="tpu_custom_call" | custom-call | flops 20000000000 | bytes 4194304 | tf_op jit(solution)/shard_map/pallas_call | solution.py:334
  25.0 1.8 %collective-permute-start = (bf16[128,512]{1,0:T(8,128)(2,1)S(1)}, bf16[128,512]{1,0:T(8,128)(2,1)S(1)}, u32[]{:S(2)}, u32[]{:S(2)}) collective-permute-start(bf16[128,512]{1,0:T(8,128)(2,1)S(1)} %get-tuple-element.10), channel_id=1, source_target_pairs={{0,16},{16,0},{1,17},{17,1},{2,18},{18,2},{3,19},{19,3},{4,20},{20... | collective-permute-start | bytes 393224 | tf_op jit(solution)/shard_map/ppermute | solution.py:365
  26.9 0.3 collective-permute-start.1
  27.1 0.0 collective-permute-done.2.refs_0_
  27.1 0.0 copy-done
  27.1 6.2 %shard_map.47.refs_2_ = bf16[4096,3072]{1,0:T(8,128)(2,1)} custom-call(bf16[128,4096]{1,0:T(8,128)(2,1)S(1)} %bitcast.6, bf16[128,1024]{1,0:T(8,128)(2,1)S(1)} %collective-permute-done.2.refs_0_, bf16[128,1792]{1,0:T(8,128)(2,1)S(1)} %get-tuple-element.13.refs_1_, bf16[256,3072]{1,0:T(8,128)(2,1)S(1)} %get-tuple-element.11.refs_2_.refs_1_, ...), custom_call_target="tpu_custom_call" | custom-call | flops 3623878656 | bytes 14155776 | tf_op jit(solution)/shard_map/pallas_call | solution.py:370
  33.4 2.3 %collective-permute-done.1.refs_0_ = bf16[128,768]{1,0:T(8,128)(2,1)S(1)} collective-permute-done((bf16[128,768]{1,0:T(8,128)(2,1)S(1)}, bf16[128,768]{1,0:T(8,128)(2,1)S(1)}, u32[]{:S(2)}, u32[]{:S(2)}) %collective-permute-start.1) | collective-permute-done | bytes 196640 | tf_op jit(solution)/shard_map/ppermute | solution.py:365
  35.7 2.6 %shard_map.48.refs_2_ = bf16[4096,3072]{1,0:T(8,128)(2,1)} custom-call(bf16[128,4096]{1,0:T(8,128)(2,1)S(1)} %bitcast.7, bf16[128,768]{1,0:T(8,128)(2,1)S(1)} %collective-permute-done.1.refs_0_, bf16[256,3072]{1,0:T(8,128)(2,1)S(1)} %get-tuple-element.11.refs_2_.refs_1_, bf16[4096,3072]{1,0:T(8,128)(2,1)} %shard_map.47.refs_2_), custom_call_target="tpu_custom_call", output_to_operand_aliasing={{}: (3, {})} | custom-call | flops 1207959552 | bytes 4718592 | tf_op jit(solution)/shard_map/pallas_call | solution.py:370
  38.3 0.0 collective-permute-done.refs_0_
  38.3 2.0 %shard_map.49 = bf16[4096,3072]{1,0:T(8,128)(2,1)} custom-call(bf16[128,4096]{1,0:T(8,128)(2,1)S(1)} %bitcast.8, bf16[128,512]{1,0:T(8,128)(2,1)S(1)} %collective-permute-done.refs_0_, bf16[256,3072]{1,0:T(8,128)(2,1)S(1)} %get-tuple-element.11.refs_2_.refs_1_, bf16[4096,3072]{1,0:T(8,128)(2,1)} %shard_map.48.refs_2_), custom_call_target="tpu_custom_call", output_to_operand_aliasing={{}: (3, {})} | custom-call | flops 805306368 | bytes 3145728 | tf_op jit(solution)/shard_map/pallas_call | solution.py:370
Async XLA Ops:
  1.0 26.2 %collective-permute-start.2 = (bf16[128,1024]{1,0:T(8,128)(2,1)S(1)}, bf16[128,1024]{1,0:T(8,128)(2,1)S(1)}, u32[]{:S(2)}, u32[]{:S(2)}) collective-permute-start(bf16[128,1024]{1,0:T(8,128)(2,1)S(1)} %slice.4), channel_id=1, source_target_pairs={{0,16},{16,0},{1,17},{17,1},{2,18},{18,2},{3,19},{19,3},{4,20},{20... | collective-permute-start | bytes 786440 | tf_op jit(solution)/shard_map/ppermute | solution.py:333
  4.0 23.1 %copy-start = (bf16[1,128,4096]{2,1,0:T(8,128)(2,1)S(1)}, bf16[1,128,4096]{2,1,0:T(8,128)(2,1)}, u32[]{:S(2)}) copy-start(bf16[1,128,4096]{2,1,0:T(8,128)(2,1)} %param.7) | copy-start | bytes 3145732
  25.0 13.2 %collective-permute-start = (bf16[128,512]{1,0:T(8,128)(2,1)S(1)}, bf16[128,512]{1,0:T(8,128)(2,1)S(1)}, u32[]{:S(2)}, u32[]{:S(2)}) collective-permute-start(bf16[128,512]{1,0:T(8,128)(2,1)S(1)} %get-tuple-element.10), channel_id=1, source_target_pairs={{0,16},{16,0},{1,17},{17,1},{2,18},{18,2},{3,19},{19,3},{4,20},{20... | collective-permute-start | bytes 393224 | tf_op jit(solution)/shard_map/ppermute | solution.py:365
  26.9 8.8 %collective-permute-start.1 = (bf16[128,768]{1,0:T(8,128)(2,1)S(1)}, bf16[128,768]{1,0:T(8,128)(2,1)S(1)}, u32[]{:S(2)}, u32[]{:S(2)}) collective-permute-start(bf16[128,768]{1,0:T(8,128)(2,1)S(1)} %get-tuple-element.12), channel_id=1, source_target_pairs={{0,16},{16,0},{1,17},{17,1},{2,18},{18,2},{3,19},{19,3},{4,20},{20... | collective-permute-start | bytes 589832 | tf_op jit(solution)/shard_map/ppermute | solution.py:365
